TPU v7x, 512 devices: a whole 4x8x8 slice. The times are simulated.
512 devices in a mesh: layer: 8 (over z), row: 16 (over y, x_hi), col: 4 (over x_lo, core).
Axes of the slice: x: 4 (x_hi: 2, x_lo: 2; x = x_hi * 2 + x_lo), y: 8, z: 8, core: 2. Of those that a mesh axis runs over, the one named last changes fastest.
Arguments:
- left_matrix: bfloat16 [8192, 16384], P('row', ('layer', 'col')), may hold values from -6 to 6
- right_matrix: bfloat16 [16384, 8192], P(('layer', 'row'), 'col'), may hold values from -0.046875 to 0.046875
Outputs:
- product: bfloat16 [8192, 8192], P(('row', 'layer'), 'col')
All inputs are finite; a program needn't handle non-finite values.
Results may differ from a plain program's by a relative error of at most 0.001.
Values may be sent and summed in bfloat16 or wider, within the bound.
No kernel may reach another device: no remote copies, remote signals or barrier semaphores. Data moves between devices by JAX's collectives and lax.ppermute only.
A program may use at most 64 MiB of HBM per device.

v0:
```python
import functools

import jax
import jax.numpy as jnp
from jax import lax
from jax.experimental import pallas as pl
from jax.experimental.pallas import tpu as pltpu
from jax.sharding import Mesh
from jax.sharding import PartitionSpec as P


ROW = ("row_0", "row_1")
LAYER_ROW = ("layer", "row_0", "row_1")
ROW_LAYER = ("row_0", "row_1", "layer")
COL = ("col_0", "col_1")
CORE = "col_1"
X = ("row_1", "col_0")
Y = ("row_0",)
Z = ("layer",)
PLACES_Y = (0, 1, 4, 5, 7, 6, 3, 2)


def ring_size(axes):
    size = 1
    for axis in axes:
        size *= lax.axis_size(axis)
    return size


def turn(place):
    return 1 - 2 * (place % 2)


def exchange(value, axes, onward):
    size = ring_size(axes)
    pairs = []
    for at in range(size):
        for core in range(2):
            place = (at - core) % size
            to = place + turn(place) if onward else place - turn(place)
            pairs.append((at * 2 + core, (to + core) % size * 2 + core))
    return lax.ppermute(value, (*axes, CORE), pairs)


def swap_cores(value):
    return lax.ppermute(value, (CORE,), [(0, 1), (1, 0)])


def place_of(axes, core):
    size = ring_size(axes)
    place = lax.rem(lax.axis_index(axes) - core + size, size)
    return place, 1 - 2 * lax.rem(place, 2)


def swap_high(value):
    return lax.ppermute(value, ("row_1",), [(0, 1), (1, 0)])


def entry(table, at):
    value = table[0]
    for index in range(1, len(table)):
        value = jnp.where(at == index, table[index], value)
    return value


def order_kernel(mine, theirs, out, sem):
    core = lax.axis_index(CORE)
    high = lax.axis_index("row_1")
    layer, s = place_of(Z, core)
    slots = (4 + s, 4, 2 * s, 3 * s, -s, -2 * s, 0, s)
    layers = [lax.rem(layer + core + slot + 16, 8) for slot in slots]
    at, u = place_of(Y, core)
    edge = mine.shape[1]
    piece = edge // 8
    for source, of in ((mine, core), (theirs, 1 - core)):
        there, t = place_of(X, of)
        for number, by in enumerate((0, t, -t, -2 * t)):
            x = lax.rem(there + of + by + 8, 4)
            other = lax.rem(x // 2 + high, 2)
            for side in range(2):
                y = (lax.rem(x, 2) * 2 + of) * 2 + side
                column = entry(PLACES_Y, lax.rem((y - core - at) * u + 16, 8)) * (edge // 2)
                for slot in range(8):
                    pltpu.make_async_copy(
                        source.at[pl.ds(pl.multiple_of(number * edge + layers[slot] * piece, piece), piece), pl.ds(side * (edge // 2), edge // 2)],
                        out.at[pl.ds(pl.multiple_of((slot * 2 + other) * piece, piece), piece), pl.ds(pl.multiple_of(column, edge // 2), edge // 2)],
                        sem,
                    ).start()
    pltpu.make_async_copy(out, out, sem).wait()


def ordered(mine, theirs):
    return pl.pallas_call(
        order_kernel,
        out_shape=pltpu.VMEM((mine.shape[0] // 2, mine.shape[1] * 4), mine.dtype),
        in_specs=[pl.BlockSpec(memory_space=pltpu.HBM)] * 2,
        out_specs=pl.BlockSpec(memory_space=pltpu.VMEM),
        scratch_shapes=[pltpu.SemaphoreType.DMA],
        cost_estimate=pl.CostEstimate(flops=1 << 30, transcendentals=0, bytes_accessed=4 * mine.size * 2),
        compiler_params=pltpu.CompilerParams(vmem_limit_bytes=8 << 20),
        name="order_left",
    )(mine, theirs)


def resident(value):
    return pltpu.with_memory_space_constraint(value, pltpu.VMEM)


IN_VMEM = pl.BlockSpec(memory_space=pltpu.VMEM)


def most_kernel(left, first, first_2, second, second_2, third, out):
    high = lax.axis_index("row_1")
    depth = third.shape[0]
    rows = left.shape[0] // 4
    block = depth // 4
    for part in range(4):
        at = pl.ds(part * rows, rows)
        total = jnp.dot(left[at, 2 * depth:3 * depth], third[...], preferred_element_type=jnp.float32)
        for number, pair in enumerate(((first, first_2), (second, second_2))):
            for side in range(2):
                for of in range(2):
                    column = number * depth + side * 2 * block + lax.rem(high + of, 2) * block
                    total += jnp.dot(left[at, pl.ds(pl.multiple_of(column, block), block)], pair[of][side * block:(side + 1) * block, :], preferred_element_type=jnp.float32)
        out[at, :] = total


def most(left, rights):
    rows = left.shape[0]
    depth, width = rights[-1].shape
    return pl.pallas_call(
        most_kernel,
        out_shape=pltpu.VMEM((rows, width), jnp.float32),
        in_specs=[IN_VMEM] * 6,
        out_specs=IN_VMEM,
        cost_estimate=pl.CostEstimate(flops=6 * rows * depth * width, transcendentals=0, bytes_accessed=4 * rows * width),
        compiler_params=pltpu.CompilerParams(vmem_limit_bytes=16 << 20),
        name="most",
    )(resident(left), *[resident(right) for right in rights])


def last_kernel(first, count, total, left, right, out):
    rows = total.shape[0] // 4
    depth = right.shape[0]
    for part in range(count):
        at = pl.ds((first + part) * rows, rows)
        out[part * rows:(part + 1) * rows, :] = total[at, :] + jnp.dot(left[at, 3 * depth:], right[...], preferred_element_type=jnp.float32)


def last(total, left, right, first, count):
    rows, width = total.shape
    depth = right.shape[0]
    return pl.pallas_call(
        functools.partial(last_kernel, first, count),
        out_shape=pltpu.VMEM((rows // 4 * count, width), jnp.float32),
        in_specs=[IN_VMEM] * 3,
        out_specs=IN_VMEM,
        cost_estimate=pl.CostEstimate(flops=rows // 2 * count * depth * width, transcendentals=0, bytes_accessed=2 * count * rows * width),
        compiler_params=pltpu.CompilerParams(vmem_limit_bytes=16 << 20),
        name="last",
    )(resident(total), resident(left), resident(right))


def step(left_matrix, right_matrix):
    high = lax.axis_index("row_1")
    depth, width = right_matrix.shape
    half = width // 2
    mine = lax.dynamic_slice(right_matrix, (0, high * half), (depth, half))
    theirs = lax.dynamic_slice(right_matrix, (0, (1 - high) * half), (depth, half))
    came = swap_high(theirs)
    near = exchange(mine, Y, True)
    first = jnp.concatenate([mine, near], axis=0)
    second = exchange(first, Y, False)
    near_came = exchange(came, Y, True)
    left_matrix, came = lax.optimization_barrier((left_matrix, came))
    first_2 = jnp.concatenate([came, near_came], axis=0)
    second_2 = exchange(first_2, Y, False)
    left_near = exchange(left_matrix, X, True)
    left_own = jnp.concatenate([left_matrix, left_near], axis=0)
    left_far = exchange(left_own, X, False)
    block = depth
    lower = jnp.where(high == 0, second, second_2)
    upper = jnp.where(high == 0, second_2, second)
    third_sent = jnp.concatenate([lower[:block], upper[:block], lower[block:], upper[block:]], axis=0)
    third = exchange(third_sent, Y, True)
    left_mine = jnp.concatenate([left_own, left_far], axis=0)
    left_theirs = swap_cores(left_mine)
    fourth = exchange(third, Y, False)
    left = ordered(left_mine, left_theirs)
    total = most(left, (first, first_2, second, second_2, third))
    away = last(total, left, fourth, 0, 1)
    rest = last(total, left, fourth, 1, 3)
    rows = away.shape[0]
    far, close, own = rest[:rows], rest[rows:2 * rows], rest[2 * rows:]
    far = far + exchange(away, Z, False)
    close = close + exchange(far, Z, True)
    own = own + exchange(close, Z, False)
    part = rows // 4
    out_sent = (own[part:2 * part] + exchange(own[3 * part:], Z, True)).astype(jnp.bfloat16)
    out_came = swap_high(out_sent)
    kept = (own[:part] + exchange(own[2 * part:3 * part], Z, True)).astype(jnp.bfloat16)
    return jnp.concatenate([jnp.where(high == 0, kept, out_came), jnp.where(high == 0, out_came, kept)], axis=1)


def solution(mesh):
    split = Mesh(
        mesh.devices.reshape(mesh.shape["layer"], 8, 2, 2, 2),
        ("layer", "row_0", "row_1", "col_0", "col_1"),
    )
    in_specs = (P(ROW, ("layer", *COL)), P(LAYER_ROW, COL))
    out_specs = P(ROW_LAYER, COL)
    return jax.shard_map(step, mesh=split, in_specs=in_specs, out_specs=out_specs, check_vma=False)
```

profile of v0, /device:TPU:56, one launch (start us, length us, event | category | flops | bytes accessed | tf_op | source)
XLA Modules:
  0.0 163.3 jit_solution(3505956538695361256)
XLA Ops:
  1.1 4.9 %collective-permute-start = (bf16[128,1024]{1,0:T(8,128)(2,1)S(1)}, bf16[128,1024]{1,0:T(8,128)(2,1)S(1)}, u32[]{:S(2)}, u32[]{:S(2)}) collective-permute-start(bf16[128,1024]{1,0:T(8,128)(2,1)S(1)} %get-tuple-element.20), channel_id=1, source_target_pairs={{0,4},{4,0},{1,5},{5,1},{2,6},{6,2},{3,7},{7,3},{8,12},{12,8},{9,1... | collective-permute-start | bytes 786440 | tf_op jit(solution)/shard_map/ppermute | solution.py:56
  6.0 6.5 %collective-permute-done = bf16[128,1024]{1,0:T(8,128)(2,1)S(1)} collective-permute-done((bf16[128,1024]{1,0:T(8,128)(2,1)S(1)}, bf16[128,1024]{1,0:T(8,128)(2,1)S(1)}, u32[]{:S(2)}, u32[]{:S(2)}) %collective-permute-start) | collective-permute-done | bytes 262176 | tf_op jit(solution)/shard_map/ppermute | solution.py:56
  12.5 3.4 %collective-permute-start.1 = (bf16[512,512]{1,0:T(8,128)(2,1)}, bf16[512,512]{1,0:T(8,128)(2,1)S(1)}, u32[]{:S(2)}, u32[]{:S(2)}) collective-permute-start(bf16[512,512]{1,0:T(8,128)(2,1)} %param.2), channel_id=1, source_target_pairs={{0,2},{1,7},{2,0},{3,5},{4,6},{5,3},{6,4},{7,1},{8,10},{9,15},{10,... | collective-permute-start | bytes 1572872 | tf_op jit(solution)/shard_map/ppermute | solution.py:42
  15.9 3.4 %collective-permute-start.4 = (bf16[128,1024]{1,0:T(8,128)(2,1)S(1)}, bf16[128,1024]{1,0:T(8,128)(2,1)S(1)}, u32[]{:S(2)}, u32[]{:S(2)}) collective-permute-start(bf16[128,1024]{1,0:T(8,128)(2,1)S(1)} %get-tuple-element.19), channel_id=1, source_target_pairs={{0,8},{1,57},{8,0},{9,17},{16,24},{17,9},{24,16},{25,33},{32,40},{... | collective-permute-start | bytes 786440 | tf_op jit(solution)/shard_map/ppermute | solution.py:42
  19.3 2.6 %collective-permute-start.5 = (bf16[128,1024]{1,0:T(8,128)(2,1)S(1)}, bf16[128,1024]{1,0:T(8,128)(2,1)S(1)}, u32[]{:S(2)}, u32[]{:S(2)}) collective-permute-start(bf16[128,1024]{1,0:T(8,128)(2,1)S(1)} %collective-permute-done), channel_id=1, source_target_pairs={{0,8},{1,57},{8,0},{9,17},{16,24},{17,9},{24,16},{25,33},{32,40},{... | collective-permute-start | bytes 786440 | tf_op jit(solution)/shard_map/ppermute | solution.py:42
  23.8 2.1 %pad_maximum_fusion = bf16[1024,512]{1,0:T(8,128)(2,1)} fusion(bf16[512,512]{1,0:T(8,128)(2,1)S(1)} %collective-permute-done.1, bf16[512,512]{1,0:T(8,128)(2,1)} %param.2), kind=kLoop, calls=%fused_computation.3 | loop fusion | flops 2097152 | bytes 2097152 | tf_op jit(solution)/shard_map/concatenate | solution.py:179
  25.9 4.7 %collective-permute-start.2 = (bf16[1024,512]{1,0:T(8,128)(2,1)}, bf16[1024,512]{1,0:T(8,128)(2,1)}, u32[]{:S(2)}, u32[]{:S(2)}) collective-permute-start(bf16[1024,512]{1,0:T(8,128)(2,1)} %pad_maximum_fusion), channel_id=1, source_target_pairs={{0,6},{1,3},{2,4},{3,1},{4,2},{5,7},{6,0},{7,5},{8,14},{9,11},{10,... | collective-permute-start | bytes 3145736 | tf_op jit(solution)/shard_map/ppermute | solution.py:42
  30.6 2.6 %collective-permute-start.6 = (bf16[256,1024]{1,0:T(8,128)(2,1)S(1)}, bf16[256,1024]{1,0:T(8,128)(2,1)S(1)}, u32[]{:S(2)}, u32[]{:S(2)}) collective-permute-start(bf16[256,1024]{1,0:T(8,128)(2,1)S(1)} %pad_maximum_fusion.2.first), channel_id=1, source_target_pairs={{0,56},{1,9},{8,16},{9,1},{16,8},{17,25},{24,32},{25,17},{32,24},{... | collective-permute-start | bytes 1572872 | tf_op jit(solution)/shard_map/ppermute | solution.py:42
  33.3 4.5 %collective-permute-start.7 = (bf16[256,1024]{1,0:T(8,128)(2,1)S(1)}, bf16[256,1024]{1,0:T(8,128)(2,1)S(1)}, u32[]{:S(2)}, u32[]{:S(2)}) collective-permute-start(bf16[256,1024]{1,0:T(8,128)(2,1)S(1)} %constant_dynamic-update-slice_fusion.3.first_2), channel_id=1, source_target_pairs={{0,56},{1,9},{8,16},{9,1},{16,8},{17,25},{24,32},{25,17},{32,24},{... | collective-permute-start | bytes 1572872 | tf_op jit(solution)/shard_map/ppermute | solution.py:42
  37.8 5.0 %collective-permute-done.6.second = bf16[256,1024]{1,0:T(8,128)(2,1)S(1)} collective-permute-done((bf16[256,1024]{1,0:T(8,128)(2,1)S(1)}, bf16[256,1024]{1,0:T(8,128)(2,1)S(1)}, u32[]{:S(2)}, u32[]{:S(2)}) %collective-permute-start.6) | collective-permute-done | bytes 524320 | tf_op jit(solution)/shard_map/ppermute | solution.py:42
  42.9 5.6 %collective-permute-done.7.second_2 = bf16[256,1024]{1,0:T(8,128)(2,1)S(1)} collective-permute-done((bf16[256,1024]{1,0:T(8,128)(2,1)S(1)}, bf16[256,1024]{1,0:T(8,128)(2,1)S(1)}, u32[]{:S(2)}, u32[]{:S(2)}) %collective-permute-start.7) | collective-permute-done | bytes 524320 | tf_op jit(solution)/shard_map/ppermute | solution.py:42
  54.0 14.6 %collective-permute-done.8.third = bf16[512,1024]{1,0:T(8,128)(2,1)S(1)} collective-permute-done((bf16[512,1024]{1,0:T(8,128)(2,1)S(1)}, bf16[512,1024]{1,0:T(8,128)(2,1)S(1)}, u32[]{:S(2)}, u32[]{:S(2)}) %collective-permute-start.8) | collective-permute-done | bytes 1048608 | tf_op jit(solution)/shard_map/ppermute | solution.py:42
  68.7 2.6 %collective-permute-start.9 = (bf16[512,1024]{1,0:T(8,128)(2,1)S(1)}, bf16[512,1024]{1,0:T(8,128)(2,1)S(1)}, u32[]{:S(2)}, u32[]{:S(2)}) collective-permute-start(bf16[512,1024]{1,0:T(8,128)(2,1)S(1)} %collective-permute-done.8.third), channel_id=1, source_target_pairs={{0,56},{1,9},{8,16},{9,1},{16,8},{17,25},{24,32},{25,17},{32,24},{... | collective-permute-start | bytes 3145736 | tf_op jit(solution)/shard_map/ppermute | solution.py:42
  72.8 5.6 %most.1.total = f32[1024,1024]{1,0:T(8,128)S(1)} custom-call(bf16[1024,2048]{1,0:T(8,128)(2,1)S(1)} %order_left.1.left, bf16[256,1024]{1,0:T(8,128)(2,1)S(1)} %pad_maximum_fusion.2.first, bf16[256,1024]{1,0:T(8,128)(2,1)S(1)} %constant_dynamic-update-slice_fusion.3.first_2, bf16[256,1024]{1,0:T(8,128)(2,1)S(1)} %collective-permute-done.6.second, ...), custom_call_target="tpu_custom_call" | custom-call | flops 3221225472 | bytes 4194304 | tf_op jit(solution)/shard_map/most/pallas_call | solution.py:131
  78.4 8.2 %collective-permute-done.9.right = bf16[512,1024]{1,0:T(8,128)(2,1)S(1)} collective-permute-done((bf16[512,1024]{1,0:T(8,128)(2,1)S(1)}, bf16[512,1024]{1,0:T(8,128)(2,1)S(1)}, u32[]{:S(2)}, u32[]{:S(2)}) %collective-permute-start.9) | collective-permute-done | bytes 1048608 | tf_op jit(solution)/shard_map/ppermute | solution.py:42
  87.0 10.9 %collective-permute-start.10 = (f32[256,1024]{1,0:T(8,128)S(1)}, f32[256,1024]{1,0:T(8,128)S(1)}, u32[]{:S(2)}, u32[]{:S(2)}) collective-permute-start(f32[256,1024]{1,0:T(8,128)S(1)} %last.3), channel_id=1, source_target_pairs={{0,448},{1,65},{64,128},{65,1},{128,64},{129,193},{192,256},{193,1... | collective-permute-start | bytes 3145736 | tf_op jit(solution)/shard_map/ppermute | solution.py:42
  99.0 11.8 %collective-permute-done.10 = f32[256,1024]{1,0:T(8,128)S(1)} collective-permute-done((f32[256,1024]{1,0:T(8,128)S(1)}, f32[256,1024]{1,0:T(8,128)S(1)}, u32[]{:S(2)}, u32[]{:S(2)}) %collective-permute-start.10) | collective-permute-done | bytes 1048608 | tf_op jit(solution)/shard_map/ppermute | solution.py:42
  112.8 14.8 %collective-permute-done.11 = f32[256,1024]{1,0:T(8,128)S(1)} collective-permute-done((f32[256,1024]{1,0:T(8,128)S(1)}, f32[256,1024]{1,0:T(8,128)S(1)}, u32[]{:S(2)}, u32[]{:S(2)}) %collective-permute-start.11) | collective-permute-done | bytes 1048608 | tf_op jit(solution)/shard_map/ppermute | solution.py:42
  127.7 5.1 %collective-permute-start.12 = (f32[256,1024]{1,0:T(8,128)S(1)}, f32[256,1024]{1,0:T(8,128)S(1)}, u32[]{:S(2)}, u32[]{:S(2)}) collective-permute-start(f32[256,1024]{1,0:T(8,128)S(1)} %slice_add_fusion.1), channel_id=1, source_target_pairs={{0,448},{1,65},{64,128},{65,1},{128,64},{129,193},{192,256},{193,1... | collective-permute-start | bytes 3145736 | tf_op jit(solution)/shard_map/ppermute | solution.py:42
  132.9 12.8 %collective-permute-done.12 = f32[256,1024]{1,0:T(8,128)S(1)} collective-permute-done((f32[256,1024]{1,0:T(8,128)S(1)}, f32[256,1024]{1,0:T(8,128)S(1)}, u32[]{:S(2)}, u32[]{:S(2)}) %collective-permute-start.12) | collective-permute-done | bytes 1048608 | tf_op jit(solution)/shard_map/ppermute | solution.py:42
  147.8 3.9 %collective-permute-start.13 = (f32[64,1024]{1,0:T(8,128)S(1)}, f32[64,1024]{1,0:T(8,128)S(1)}, u32[]{:S(2)}, u32[]{:S(2)}) collective-permute-start(f32[64,1024]{1,0:T(8,128)S(1)} %get-tuple-element.11), channel_id=1, source_target_pairs={{0,64},{1,449},{64,0},{65,129},{128,192},{129,65},{192,128},{193,2... | collective-permute-start | bytes 786440 | tf_op jit(solution)/shard_map/ppermute | solution.py:42
  151.7 2.4 %collective-permute-done.14 = f32[64,1024]{1,0:T(8,128)S(1)} collective-permute-done((f32[64,1024]{1,0:T(8,128)S(1)}, f32[64,1024]{1,0:T(8,128)S(1)}, u32[]{:S(2)}, u32[]{:S(2)}) %collective-permute-start.14) | collective-permute-done | bytes 262176 | tf_op jit(solution)/shard_map/ppermute | solution.py:42
  154.1 2.7 %collective-permute-start.15 = (bf16[64,1024]{1,0:T(8,128)(2,1)S(1)}, bf16[64,1024]{1,0:T(8,128)(2,1)S(1)}, u32[]{:S(2)}, u32[]{:S(2)}) collective-permute-start(bf16[64,1024]{1,0:T(8,128)(2,1)S(1)} %fusion), channel_id=1, source_target_pairs={{0,4},{4,0},{1,5},{5,1},{2,6},{6,2},{3,7},{7,3},{8,12},{12,8},{9,1... | collective-permute-start | bytes 393224 | tf_op jit(solution)/shard_map/ppermute | solution.py:56
  156.9 5.6 %collective-permute-done.15 = bf16[64,1024]{1,0:T(8,128)(2,1)S(1)} collective-permute-done((bf16[64,1024]{1,0:T(8,128)(2,1)S(1)}, bf16[64,1024]{1,0:T(8,128)(2,1)S(1)}, u32[]{:S(2)}, u32[]{:S(2)}) %collective-permute-start.15) | collective-permute-done | bytes 131104 | tf_op jit(solution)/shard_map/ppermute | solution.py:56
  (33 shorter events, 16.7 us)
Async XLA Ops:
  1.1 11.4 %collective-permute-start = (bf16[128,1024]{1,0:T(8,128)(2,1)S(1)}, bf16[128,1024]{1,0:T(8,128)(2,1)S(1)}, u32[]{:S(2)}, u32[]{:S(2)}) collective-permute-start(bf16[128,1024]{1,0:T(8,128)(2,1)S(1)} %get-tuple-element.20), channel_id=1, source_target_pairs={{0,4},{4,0},{1,5},{5,1},{2,6},{6,2},{3,7},{7,3},{8,12},{12,8},{9,1... | collective-permute-start | bytes 786440 | tf_op jit(solution)/shard_map/ppermute | solution.py:56
  12.5 11.3 %collective-permute-start.1 = (bf16[512,512]{1,0:T(8,128)(2,1)}, bf16[512,512]{1,0:T(8,128)(2,1)S(1)}, u32[]{:S(2)}, u32[]{:S(2)}) collective-permute-start(bf16[512,512]{1,0:T(8,128)(2,1)} %param.2), channel_id=1, source_target_pairs={{0,2},{1,7},{2,0},{3,5},{4,6},{5,3},{6,4},{7,1},{8,10},{9,15},{10,... | collective-permute-start | bytes 1572872 | tf_op jit(solution)/shard_map/ppermute | solution.py:42
  15.9 21.8 %copy-start = (bf16[512,512]{1,0:T(8,128)(2,1)S(1)}, bf16[512,512]{1,0:T(8,128)(2,1)}, u32[]{:S(2)}) copy-start(bf16[512,512]{1,0:T(8,128)(2,1)} %param.2) | copy-start | bytes 1572868
  15.9 14.6 %collective-permute-start.4 = (bf16[128,1024]{1,0:T(8,128)(2,1)S(1)}, bf16[128,1024]{1,0:T(8,128)(2,1)S(1)}, u32[]{:S(2)}, u32[]{:S(2)}) collective-permute-start(bf16[128,1024]{1,0:T(8,128)(2,1)S(1)} %get-tuple-element.19), channel_id=1, source_target_pairs={{0,8},{1,57},{8,0},{9,17},{16,24},{17,9},{24,16},{25,33},{32,40},{... | collective-permute-start | bytes 786440 | tf_op jit(solution)/shard_map/ppermute | solution.py:42
  19.3 13.9 %collective-permute-start.5 = (bf16[128,1024]{1,0:T(8,128)(2,1)S(1)}, bf16[128,1024]{1,0:T(8,128)(2,1)S(1)}, u32[]{:S(2)}, u32[]{:S(2)}) collective-permute-start(bf16[128,1024]{1,0:T(8,128)(2,1)S(1)} %collective-permute-done), channel_id=1, source_target_pairs={{0,8},{1,57},{8,0},{9,17},{16,24},{17,9},{24,16},{25,33},{32,40},{... | collective-permute-start | bytes 786440 | tf_op jit(solution)/shard_map/ppermute | solution.py:42
  25.9 22.7 %collective-permute-start.2 = (bf16[1024,512]{1,0:T(8,128)(2,1)}, bf16[1024,512]{1,0:T(8,128)(2,1)}, u32[]{:S(2)}, u32[]{:S(2)}) collective-permute-start(bf16[1024,512]{1,0:T(8,128)(2,1)} %pad_maximum_fusion), channel_id=1, source_target_pairs={{0,6},{1,3},{2,4},{3,1},{4,2},{5,7},{6,0},{7,5},{8,14},{9,11},{10,... | collective-permute-start | bytes 3145736 | tf_op jit(solution)/shard_map/ppermute | solution.py:42
  30.6 12.3 %collective-permute-start.6 = (bf16[256,1024]{1,0:T(8,128)(2,1)S(1)}, bf16[256,1024]{1,0:T(8,128)(2,1)S(1)}, u32[]{:S(2)}, u32[]{:S(2)}) collective-permute-start(bf16[256,1024]{1,0:T(8,128)(2,1)S(1)} %pad_maximum_fusion.2.first), channel_id=1, source_target_pairs={{0,56},{1,9},{8,16},{9,1},{16,8},{17,25},{24,32},{25,17},{32,24},{... | collective-permute-start | bytes 1572872 | tf_op jit(solution)/shard_map/ppermute | solution.py:42
  33.3 15.2 %collective-permute-start.7 = (bf16[256,1024]{1,0:T(8,128)(2,1)S(1)}, bf16[256,1024]{1,0:T(8,128)(2,1)S(1)}, u32[]{:S(2)}, u32[]{:S(2)}) collective-permute-start(bf16[256,1024]{1,0:T(8,128)(2,1)S(1)} %constant_dynamic-update-slice_fusion.3.first_2), channel_id=1, source_target_pairs={{0,56},{1,9},{8,16},{9,1},{16,8},{17,25},{24,32},{25,17},{32,24},{... | collective-permute-start | bytes 1572872 | tf_op jit(solution)/shard_map/ppermute | solution.py:42
  49.9 21.4 %collective-permute-start.3 = (bf16[2048,512]{1,0:T(8,128)(2,1)S(1)}, bf16[2048,512]{1,0:T(8,128)(2,1)S(1)}, u32[]{:S(2)}, u32[]{:S(2)}) collective-permute-start(bf16[2048,512]{1,0:T(8,128)(2,1)S(1)} %constant_dynamic-update-slice_fusion.mine), channel_id=1, source_target_pairs={{0,1},{1,0},{2,3},{3,2},{4,5},{5,4},{6,7},{7,6},{8,9},{9,8},{10,11... | collective-permute-start | bytes 6291464 | tf_op jit(solution)/shard_map/ppermute | solution.py:46
  52.0 16.7 %collective-permute-start.8 = (bf16[512,1024]{1,0:T(8,128)(2,1)S(1)}, bf16[512,1024]{1,0:T(8,128)(2,1)S(1)}, u32[]{:S(2)}, u32[]{:S(2)}) collective-permute-start(bf16[512,1024]{1,0:T(8,128)(2,1)S(1)} %pad_maximum_fusion.1), channel_id=1, source_target_pairs={{0,8},{1,57},{8,0},{9,17},{16,24},{17,9},{24,16},{25,33},{32,40},{... | collective-permute-start | bytes 3145736 | tf_op jit(solution)/shard_map/ppermute | solution.py:42
  68.7 17.9 %collective-permute-start.9 = (bf16[512,1024]{1,0:T(8,128)(2,1)S(1)}, bf16[512,1024]{1,0:T(8,128)(2,1)S(1)}, u32[]{:S(2)}, u32[]{:S(2)}) collective-permute-start(bf16[512,1024]{1,0:T(8,128)(2,1)S(1)} %collective-permute-done.8.third), channel_id=1, source_target_pairs={{0,56},{1,9},{8,16},{9,1},{16,8},{17,25},{24,32},{25,17},{32,24},{... | collective-permute-start | bytes 3145736 | tf_op jit(solution)/shard_map/ppermute | solution.py:42
  87.0 23.7 %collective-permute-start.10 = (f32[256,1024]{1,0:T(8,128)S(1)}, f32[256,1024]{1,0:T(8,128)S(1)}, u32[]{:S(2)}, u32[]{:S(2)}) collective-permute-start(f32[256,1024]{1,0:T(8,128)S(1)} %last.3), channel_id=1, source_target_pairs={{0,448},{1,65},{64,128},{65,1},{128,64},{129,193},{192,256},{193,1... | collective-permute-start | bytes 3145736 | tf_op jit(solution)/shard_map/ppermute | solution.py:42
  110.9 16.7 %collective-permute-start.11 = (f32[256,1024]{1,0:T(8,128)S(1)}, f32[256,1024]{1,0:T(8,128)S(1)}, u32[]{:S(2)}, u32[]{:S(2)}) collective-permute-start(f32[256,1024]{1,0:T(8,128)S(1)} %slice_add_fusion), channel_id=1, source_target_pairs={{0,64},{1,449},{64,0},{65,129},{128,192},{129,65},{192,128},{193,2... | collective-permute-start | bytes 3145736 | tf_op jit(solution)/shard_map/ppermute | solution.py:42
  127.7 17.9 %collective-permute-start.12 = (f32[256,1024]{1,0:T(8,128)S(1)}, f32[256,1024]{1,0:T(8,128)S(1)}, u32[]{:S(2)}, u32[]{:S(2)}) collective-permute-start(f32[256,1024]{1,0:T(8,128)S(1)} %slice_add_fusion.1), channel_id=1, source_target_pairs={{0,448},{1,65},{64,128},{65,1},{128,64},{129,193},{192,256},{193,1... | collective-permute-start | bytes 3145736 | tf_op jit(solution)/shard_map/ppermute | solution.py:42
  145.8 8.3 %collective-permute-start.14 = (f32[64,1024]{1,0:T(8,128)S(1)}, f32[64,1024]{1,0:T(8,128)S(1)}, u32[]{:S(2)}, u32[]{:S(2)}) collective-permute-start(f32[64,1024]{1,0:T(8,128)S(1)} %get-tuple-element.12), channel_id=1, source_target_pairs={{0,64},{1,449},{64,0},{65,129},{128,192},{129,65},{192,128},{193,2... | collective-permute-start | bytes 786440 | tf_op jit(solution)/shard_map/ppermute | solution.py:42
  147.8 9.1 %collective-permute-start.13 = (f32[64,1024]{1,0:T(8,128)S(1)}, f32[64,1024]{1,0:T(8,128)S(1)}, u32[]{:S(2)}, u32[]{:S(2)}) collective-permute-start(f32[64,1024]{1,0:T(8,128)S(1)} %get-tuple-element.11), channel_id=1, source_target_pairs={{0,64},{1,449},{64,0},{65,129},{128,192},{129,65},{192,128},{193,2... | collective-permute-start | bytes 786440 | tf_op jit(solution)/shard_map/ppermute | solution.py:42
  154.1 8.4 %collective-permute-start.15 = (bf16[64,1024]{1,0:T(8,128)(2,1)S(1)}, bf16[64,1024]{1,0:T(8,128)(2,1)S(1)}, u32[]{:S(2)}, u32[]{:S(2)}) collective-permute-start(bf16[64,1024]{1,0:T(8,128)(2,1)S(1)} %fusion), channel_id=1, source_target_pairs={{0,4},{4,0},{1,5},{5,1},{2,6},{6,2},{3,7},{7,3},{8,12},{12,8},{9,1... | collective-permute-start | bytes 393224 | tf_op jit(solution)/shard_map/ppermute | solution.py:56
where the time goes:
time: 164 us; the launch traced here: 163 us
  waiting for transfers between devices  89.2 us (54%)
  starting transfers between devices  59.1 us (36%)
  Pallas kernels  8.52 us (5%)
  other arithmetic  3.55 us (2%)
  local copies, waits for them, and re-layouts  2.59 us (2%)
    ppermute x13, waiting for transfers between devices, exchange(): return lax.ppermute(value, (*axes, CORE), pairs)  77.1 us
    ppermute x13, starting transfers between devices, exchange(): return lax.ppermute(value, (*axes, CORE), pairs)  49.6 us
    ppermute x2, waiting for transfers between devices, swap_high(): return lax.ppermute(value, ('row_1',), [(0, 1), (1, 0)])  12.1 us
    ppermute x2, starting transfers between devices, swap_high(): return lax.ppermute(value, ('row_1',), [(0, 1), (1, 0)])  7.64 us
    pallas_call x1, Pallas kernels, most(): pl.pallas_call(most_kernel, out_shape=pltpu.VMEM((rows, width), jnp.float...  5.59 us
  transfers between devices with their start and end apart: 16, of which 12 were waited for; matrix products, arithmetic and copies ran while one was open for 2% of the time, Pallas kernels for 5%

commit v1 on v0

--- a/solution.py
+++ b/solution.py
@@ -63,43 +63,46 @@
     return value
 
 
-def order_kernel(mine, theirs, out, sem):
+def order_kernel(own, far, own_2, far_2, out, sem):
     core = lax.axis_index(CORE)
     high = lax.axis_index("row_1")
     layer, s = place_of(Z, core)
     slots = (4 + s, 4, 2 * s, 3 * s, -s, -2 * s, 0, s)
     layers = [lax.rem(layer + core + slot + 16, 8) for slot in slots]
     at, u = place_of(Y, core)
-    edge = mine.shape[1]
+    edge = own.shape[1]
     piece = edge // 8
-    for source, of in ((mine, core), (theirs, 1 - core)):
+    for sources, of in (((own, far), core), ((own_2, far_2), 1 - core)):
         there, t = place_of(X, of)
         for number, by in enumerate((0, t, -t, -2 * t)):
             x = lax.rem(there + of + by + 8, 4)
             other = lax.rem(x // 2 + high, 2)
-            for side in range(2):
-                y = (lax.rem(x, 2) * 2 + of) * 2 + side
-                column = entry(PLACES_Y, lax.rem((y - core - at) * u + 16, 8)) * (edge // 2)
+            source = sources[number // 2]
+            for quarter in range(4):
+                y = (lax.rem(x, 2) * 2 + of) * 2 + quarter // 2
+                place = entry(PLACES_Y, lax.rem((y - core - at) * u + 16, 8))
+                column = place // 2 * edge + lax.rem(high + quarter, 2) * (edge // 2) + lax.rem(place, 2) * (edge // 4)
                 for slot in range(8):
                     pltpu.make_async_copy(
-                        source.at[pl.ds(pl.multiple_of(number * edge + layers[slot] * piece, piece), piece), pl.ds(side * (edge // 2), edge // 2)],
-                        out.at[pl.ds(pl.multiple_of((slot * 2 + other) * piece, piece), piece), pl.ds(pl.multiple_of(column, edge // 2), edge // 2)],
+                        source.at[pl.ds(pl.multiple_of(number % 2 * edge + layers[slot] * piece, piece), piece), pl.ds(quarter * (edge // 4), edge // 4)],
+                        out.at[pl.ds(pl.multiple_of((slot * 2 + other) * piece, piece), piece), pl.ds(pl.multiple_of(column, edge // 4), edge // 4)],
                         sem,
                     ).start()
     pltpu.make_async_copy(out, out, sem).wait()
 
 
-def ordered(mine, theirs):
+def ordered(*pieces):
+    rows, edge = pieces[0].shape
     return pl.pallas_call(
         order_kernel,
-        out_shape=pltpu.VMEM((mine.shape[0] // 2, mine.shape[1] * 4), mine.dtype),
-        in_specs=[pl.BlockSpec(memory_space=pltpu.HBM)] * 2,
+        out_shape=pltpu.VMEM((rows, edge * 4), pieces[0].dtype),
+        in_specs=[pl.BlockSpec(memory_space=pltpu.HBM)] * 4,
         out_specs=pl.BlockSpec(memory_space=pltpu.VMEM),
         scratch_shapes=[pltpu.SemaphoreType.DMA],
-        cost_estimate=pl.CostEstimate(flops=1 << 30, transcendentals=0, bytes_accessed=4 * mine.size * 2),
+        cost_estimate=pl.CostEstimate(flops=1 << 30, transcendentals=0, bytes_accessed=16 * rows * edge),
         compiler_params=pltpu.CompilerParams(vmem_limit_bytes=8 << 20),
         name="order_left",
-    )(mine, theirs)
+    )(*pieces)
 
 
 def resident(value):
@@ -110,18 +113,16 @@
 
 
 def most_kernel(left, first, first_2, second, second_2, third, out):
-    high = lax.axis_index("row_1")
-    depth = third.shape[0]
     rows = left.shape[0] // 4
-    block = depth // 4
     for part in range(4):
         at = pl.ds(part * rows, rows)
-        total = jnp.dot(left[at, 2 * depth:3 * depth], third[...], preferred_element_type=jnp.float32)
-        for number, pair in enumerate(((first, first_2), (second, second_2))):
-            for side in range(2):
-                for of in range(2):
-                    column = number * depth + side * 2 * block + lax.rem(high + of, 2) * block
-                    total += jnp.dot(left[at, pl.ds(pl.multiple_of(column, block), block)], pair[of][side * block:(side + 1) * block, :], preferred_element_type=jnp.float32)
+        total = None
+        column = 0
+        for right in (first, first_2, second, second_2, third):
+            depth = right.shape[0]
+            term = jnp.dot(left[at, column:column + depth], right[...], preferred_element_type=jnp.float32)
+            total = term if total is None else total + term
+            column += depth
         out[at, :] = total
 
 
@@ -139,19 +140,20 @@
     )(resident(left), *[resident(right) for right in rights])
 
 
-def last_kernel(first, count, total, left, right, out):
+def last_kernel(first, count, side, total, left, right, out):
     rows = total.shape[0] // 4
     depth = right.shape[0]
     for part in range(count):
         at = pl.ds((first + part) * rows, rows)
-        out[part * rows:(part + 1) * rows, :] = total[at, :] + jnp.dot(left[at, 3 * depth:], right[...], preferred_element_type=jnp.float32)
-
-
-def last(total, left, right, first, count):
-    rows, width = total.shape
-    depth = right.shape[0]
+        width = right.shape[1]
+        out[part * rows:(part + 1) * rows, :] = total[at, side * width:(side + 1) * width] + jnp.dot(left[at, 3 * depth:], right[...], preferred_element_type=jnp.float32)
+
+
+def last(total, left, right, first, count, side):
+    rows = total.shape[0]
+    depth, width = right.shape
     return pl.pallas_call(
-        functools.partial(last_kernel, first, count),
+        functools.partial(last_kernel, first, count, side),
         out_shape=pltpu.VMEM((rows // 4 * count, width), jnp.float32),
         in_specs=[IN_VMEM] * 3,
         out_specs=IN_VMEM,
@@ -178,27 +180,30 @@
     left_near = exchange(left_matrix, X, True)
     left_own = jnp.concatenate([left_matrix, left_near], axis=0)
     left_far = exchange(left_own, X, False)
-    block = depth
-    lower = jnp.where(high == 0, second, second_2)
-    upper = jnp.where(high == 0, second_2, second)
-    third_sent = jnp.concatenate([lower[:block], upper[:block], lower[block:], upper[block:]], axis=0)
+    third_sent = jnp.concatenate([second, second_2], axis=0)
     third = exchange(third_sent, Y, True)
-    left_mine = jnp.concatenate([left_own, left_far], axis=0)
-    left_theirs = swap_cores(left_mine)
-    fourth = exchange(third, Y, False)
-    left = ordered(left_mine, left_theirs)
+    own_theirs = swap_cores(left_own)
+    far_theirs = swap_cores(left_far)
+    middle = third.shape[1] // 2
+    fourth = exchange(third[:, :middle], Y, False)
+    fourth_right = exchange(third[:, middle:], Y, False)
+    left = ordered(left_own, left_far, own_theirs, far_theirs)
     total = most(left, (first, first_2, second, second_2, third))
-    away = last(total, left, fourth, 0, 1)
-    rest = last(total, left, fourth, 1, 3)
-    rows = away.shape[0]
-    far, close, own = rest[:rows], rest[rows:2 * rows], rest[2 * rows:]
-    far = far + exchange(away, Z, False)
-    close = close + exchange(far, Z, True)
-    own = own + exchange(close, Z, False)
-    part = rows // 4
-    out_sent = (own[part:2 * part] + exchange(own[3 * part:], Z, True)).astype(jnp.bfloat16)
-    out_came = swap_high(out_sent)
-    kept = (own[:part] + exchange(own[2 * part:3 * part], Z, True)).astype(jnp.bfloat16)
+    kept = []
+    out_came = []
+    for side, columns in enumerate((fourth, fourth_right)):
+        away = last(total, left, columns, 0, 1, side)
+        rest = last(total, left, columns, 1, 3, side)
+        rows = away.shape[0]
+        far, close, own = rest[:rows], rest[rows:2 * rows], rest[2 * rows:]
+        far = far + exchange(away, Z, False)
+        close = close + exchange(far, Z, True)
+        own = own + exchange(close, Z, False)
+        own = (own[:rows // 2] + exchange(own[rows // 2:], Z, True)).astype(jnp.bfloat16)
+        kept.append(own[:rows // 4])
+        out_came.append(swap_high(own[rows // 4:]))
+    kept = jnp.concatenate(kept, axis=1)
+    out_came = jnp.concatenate(out_came, axis=1)
     return jnp.concatenate([jnp.where(high == 0, kept, out_came), jnp.where(high == 0, out_came, kept)], axis=1)
 
 

time: 164 us -> 163 us (level)
  the two profiles are of different devices: /device:TPU:56 before, /device:TPU:32 now
where the time goes in v1:
time: 163 us; the launch traced here: 162 us
  starting transfers between devices  75.2 us (46%)
  waiting for transfers between devices  72.7 us (45%)
  Pallas kernels  6.9 us (4%)
  other arithmetic  5.12 us (3%)
    ppermute x17, waiting for transfers between devices, exchange(): return lax.ppermute(value, (*axes, CORE), pairs)  63 us
    ppermute x17, starting transfers between devices, exchange(): return lax.ppermute(value, (*axes, CORE), pairs)  62.1 us
    ppermute x3, waiting for transfers between devices, swap_high(): return lax.ppermute(value, ('row_1',), [(0, 1), (1, 0)])  9.62 us
    ppermute x3, starting transfers between devices, swap_high(): return lax.ppermute(value, ('row_1',), [(0, 1), (1, 0)])  8.77 us
    ppermute x2, starting transfers between devices, swap_cores(): return lax.ppermute(value, (CORE,), [(0, 1), (1, 0)])  4.33 us
    pallas_call x1, Pallas kernels, most(): pl.pallas_call(most_kernel, out_shape=pltpu.VMEM((rows, width), jnp.float...  3.41 us
  transfers between devices with their start and end apart: 22, of which 11 were waited for; matrix products, arithmetic and copies ran while one was open for 3% of the time, Pallas kernels for 4%

profile of v1, /device:TPU:32, one launch (start us, length us, event | category | flops | bytes accessed | tf_op | source)
XLA Modules:
  0.0 161.7 jit_solution(11790558029366074142)
XLA Ops:
  1.1 4.9 %collective-permute-start = (bf16[128,1024]{1,0:T(8,128)(2,1)S(1)}, bf16[128,1024]{1,0:T(8,128)(2,1)S(1)}, u32[]{:S(2)}, u32[]{:S(2)}) collective-permute-start(bf16[128,1024]{1,0:T(8,128)(2,1)S(1)} %get-tuple-element.12), channel_id=1, source_target_pairs={{0,4},{4,0},{1,5},{5,1},{2,6},{6,2},{3,7},{7,3},{8,12},{12,8},{9,1... | collective-permute-start | bytes 786440 | tf_op jit(solution)/shard_map/ppermute | solution.py:56
  6.1 2.6 %collective-permute-start.5 = (bf16[128,1024]{1,0:T(8,128)(2,1)S(1)}, bf16[128,1024]{1,0:T(8,128)(2,1)S(1)}, u32[]{:S(2)}, u32[]{:S(2)}) collective-permute-start(bf16[128,1024]{1,0:T(8,128)(2,1)S(1)} %get-tuple-element.11), channel_id=1, source_target_pairs={{0,8},{1,57},{8,0},{9,17},{16,24},{17,9},{24,16},{25,33},{32,40},{... | collective-permute-start | bytes 786440 | tf_op jit(solution)/shard_map/ppermute | solution.py:42
  8.7 3.9 %collective-permute-done = bf16[128,1024]{1,0:T(8,128)(2,1)S(1)} collective-permute-done((bf16[128,1024]{1,0:T(8,128)(2,1)S(1)}, bf16[128,1024]{1,0:T(8,128)(2,1)S(1)}, u32[]{:S(2)}, u32[]{:S(2)}) %collective-permute-start) | collective-permute-done | bytes 262176 | tf_op jit(solution)/shard_map/ppermute | solution.py:56
  12.6 3.4 %collective-permute-start.1 = (bf16[512,512]{1,0:T(8,128)(2,1)}, bf16[512,512]{1,0:T(8,128)(2,1)S(1)}, u32[]{:S(2)}, u32[]{:S(2)}) collective-permute-start(bf16[512,512]{1,0:T(8,128)(2,1)} %param.2), channel_id=1, source_target_pairs={{0,2},{1,7},{2,0},{3,5},{4,6},{5,3},{6,4},{7,1},{8,10},{9,15},{10,... | collective-permute-start | bytes 1572872 | tf_op jit(solution)/shard_map/ppermute | solution.py:42
  16.0 2.6 %collective-permute-start.6 = (bf16[128,1024]{1,0:T(8,128)(2,1)S(1)}, bf16[128,1024]{1,0:T(8,128)(2,1)S(1)}, u32[]{:S(2)}, u32[]{:S(2)}) collective-permute-start(bf16[128,1024]{1,0:T(8,128)(2,1)S(1)} %collective-permute-done), channel_id=1, source_target_pairs={{0,8},{1,57},{8,0},{9,17},{16,24},{17,9},{24,16},{25,33},{32,40},{... | collective-permute-start | bytes 786440 | tf_op jit(solution)/shard_map/ppermute | solution.py:42
  18.6 2.1 %collective-permute-start.7 = (bf16[256,1024]{1,0:T(8,128)(2,1)S(1)}, bf16[256,1024]{1,0:T(8,128)(2,1)S(1)}, u32[]{:S(2)}, u32[]{:S(2)}) collective-permute-start(bf16[256,1024]{1,0:T(8,128)(2,1)S(1)} %pad_maximum_fusion.1.first), channel_id=1, source_target_pairs={{0,56},{1,9},{8,16},{9,1},{16,8},{17,25},{24,32},{25,17},{32,24},{... | collective-permute-start | bytes 1572872 | tf_op jit(solution)/shard_map/ppermute | solution.py:42
  20.8 5.1 %collective-permute-done.6 = bf16[128,1024]{1,0:T(8,128)(2,1)S(1)} collective-permute-done((bf16[128,1024]{1,0:T(8,128)(2,1)S(1)}, bf16[128,1024]{1,0:T(8,128)(2,1)S(1)}, u32[]{:S(2)}, u32[]{:S(2)}) %collective-permute-start.6) | collective-permute-done | bytes 262176 | tf_op jit(solution)/shard_map/ppermute | solution.py:42
  26.0 5.1 %collective-permute-start.2 = (bf16[1024,512]{1,0:T(8,128)(2,1)S(1)}, bf16[1024,512]{1,0:T(8,128)(2,1)S(1)}, u32[]{:S(2)}, u32[]{:S(2)}) collective-permute-start(bf16[1024,512]{1,0:T(8,128)(2,1)S(1)} %constant_dynamic-update-slice_fusion.own), channel_id=1, source_target_pairs={{0,6},{1,3},{2,4},{3,1},{4,2},{5,7},{6,0},{7,5},{8,14},{9,11},{10,... | collective-permute-start | bytes 3145736 | tf_op jit(solution)/shard_map/ppermute | solution.py:42
  33.1 11.5 %collective-permute-done.8.second_2 = bf16[256,1024]{1,0:T(8,128)(2,1)S(1)} collective-permute-done((bf16[256,1024]{1,0:T(8,128)(2,1)S(1)}, bf16[256,1024]{1,0:T(8,128)(2,1)S(1)}, u32[]{:S(2)}, u32[]{:S(2)}) %collective-permute-start.8) | collective-permute-done | bytes 524320 | tf_op jit(solution)/shard_map/ppermute | solution.py:42
  48.5 2.4 %collective-permute-start.4 = (bf16[1024,512]{1,0:T(8,128)(2,1)S(1)}, bf16[1024,512]{1,0:T(8,128)(2,1)S(1)}, u32[]{:S(2)}, u32[]{:S(2)}) collective-permute-start(bf16[1024,512]{1,0:T(8,128)(2,1)S(1)} %collective-permute-done.2.far), channel_id=1, source_target_pairs={{0,1},{1,0},{2,3},{3,2},{4,5},{5,4},{6,7},{7,6},{8,9},{9,8},{10,11... | collective-permute-start | bytes 3145736 | tf_op jit(solution)/shard_map/ppermute | solution.py:46
  50.9 12.7 %collective-permute-done.9.third = bf16[512,1024]{1,0:T(8,128)(2,1)S(1)} collective-permute-done((bf16[512,1024]{1,0:T(8,128)(2,1)S(1)}, bf16[512,1024]{1,0:T(8,128)(2,1)S(1)}, u32[]{:S(2)}, u32[]{:S(2)}) %collective-permute-start.9) | collective-permute-done | bytes 1048608 | tf_op jit(solution)/shard_map/ppermute | solution.py:42
  65.6 5.1 %collective-permute-start.15 = (bf16[512,512]{1,0:T(8,128)(2,1)S(1)}, bf16[512,512]{1,0:T(8,128)(2,1)S(1)}, u32[]{:S(2)}, u32[]{:S(2)}) collective-permute-start(bf16[512,512]{1,0:T(8,128)(2,1)S(1)} %get-tuple-element.9), channel_id=1, source_target_pairs={{0,56},{1,9},{8,16},{9,1},{16,8},{17,25},{24,32},{25,17},{32,24},{... | collective-permute-start | bytes 1572872 | tf_op jit(solution)/shard_map/ppermute | solution.py:42
  72.6 3.4 %most.1.total = f32[1024,1024]{1,0:T(8,128)S(1)} custom-call(bf16[1024,2048]{1,0:T(8,128)(2,1)S(1)} %order_left.1.left, bf16[256,1024]{1,0:T(8,128)(2,1)S(1)} %pad_maximum_fusion.1.first, bf16[256,1024]{1,0:T(8,128)(2,1)S(1)} %constant_dynamic-update-slice_fusion.2.first_2, bf16[256,1024]{1,0:T(8,128)(2,1)S(1)} %collective-permute-done.7.second, ...), custom_call_target="tpu_custom_call" | custom-call | flops 3221225472 | bytes 4194304 | tf_op jit(solution)/shard_map/most/pallas_call | solution.py:132
  76.3 10.9 %collective-permute-start.11 = (f32[256,512]{1,0:T(8,128)S(1)}, f32[256,512]{1,0:T(8,128)S(1)}, u32[]{:S(2)}, u32[]{:S(2)}) collective-permute-start(f32[256,512]{1,0:T(8,128)S(1)} %last.5), channel_id=1, source_target_pairs={{0,448},{1,65},{64,128},{65,1},{128,64},{129,193},{192,256},{193,1... | collective-permute-start | bytes 1572872 | tf_op jit(solution)/shard_map/ppermute | solution.py:42
  87.6 5.3 %collective-permute-start.16 = (f32[256,512]{1,0:T(8,128)S(1)}, f32[256,512]{1,0:T(8,128)S(1)}, u32[]{:S(2)}, u32[]{:S(2)}) collective-permute-start(f32[256,512]{1,0:T(8,128)S(1)} %last.7), channel_id=1, source_target_pairs={{0,448},{1,65},{64,128},{65,1},{128,64},{129,193},{192,256},{193,1... | collective-permute-start | bytes 1572872 | tf_op jit(solution)/shard_map/ppermute | solution.py:42
  93.4 6.2 %collective-permute-done.11 = f32[256,512]{1,0:T(8,128)S(1)} collective-permute-done((f32[256,512]{1,0:T(8,128)S(1)}, f32[256,512]{1,0:T(8,128)S(1)}, u32[]{:S(2)}, u32[]{:S(2)}) %collective-permute-start.11) | collective-permute-done | bytes 524320 | tf_op jit(solution)/shard_map/ppermute | solution.py:42
  102.2 8.6 %collective-permute-done.16 = f32[256,512]{1,0:T(8,128)S(1)} collective-permute-done((f32[256,512]{1,0:T(8,128)S(1)}, f32[256,512]{1,0:T(8,128)S(1)}, u32[]{:S(2)}, u32[]{:S(2)}) %collective-permute-start.16) | collective-permute-done | bytes 524320 | tf_op jit(solution)/shard_map/ppermute | solution.py:42
  112.9 2.6 %collective-permute-done.12 = f32[256,512]{1,0:T(8,128)S(1)} collective-permute-done((f32[256,512]{1,0:T(8,128)S(1)}, f32[256,512]{1,0:T(8,128)S(1)}, u32[]{:S(2)}, u32[]{:S(2)}) %collective-permute-start.12) | collective-permute-done | bytes 524320 | tf_op jit(solution)/shard_map/ppermute | solution.py:42
  116.3 6.0 %collective-permute-start.13 = (f32[256,512]{1,0:T(8,128)}, f32[256,512]{1,0:T(8,128)}, u32[]{:S(2)}, u32[]{:S(2)}) collective-permute-start(f32[256,512]{1,0:T(8,128)} %slice_add_fusion.4), channel_id=1, source_target_pairs={{0,448},{1,65},{64,128},{65,1},{128,64},{129,193},{192,256},{193,1... | collective-permute-start | bytes 1572872 | tf_op jit(solution)/shard_map/ppermute | solution.py:42
  122.3 5.1 %collective-permute-done.17 = f32[256,512]{1,0:T(8,128)S(1)} collective-permute-done((f32[256,512]{1,0:T(8,128)S(1)}, f32[256,512]{1,0:T(8,128)S(1)}, u32[]{:S(2)}, u32[]{:S(2)}) %collective-permute-start.17) | collective-permute-done | bytes 524320 | tf_op jit(solution)/shard_map/ppermute | solution.py:42
  128.3 5.5 %collective-permute-start.18 = (f32[256,512]{1,0:T(8,128)}, f32[256,512]{1,0:T(8,128)}, u32[]{:S(2)}, u32[]{:S(2)}) collective-permute-start(f32[256,512]{1,0:T(8,128)} %slice_add_fusion.1), channel_id=1, source_target_pairs={{0,448},{1,65},{64,128},{65,1},{128,64},{129,193},{192,256},{193,1... | collective-permute-start | bytes 1572872 | tf_op jit(solution)/shard_map/ppermute | solution.py:42
  136.9 6.9 %collective-permute-done.18 = f32[256,512]{1,0:T(8,128)} collective-permute-done((f32[256,512]{1,0:T(8,128)}, f32[256,512]{1,0:T(8,128)}, u32[]{:S(2)}, u32[]{:S(2)}) %collective-permute-start.18) | collective-permute-done | bytes 524320 | tf_op jit(solution)/shard_map/ppermute | solution.py:42
  148.9 4.3 %collective-permute-done.19 = f32[128,512]{1,0:T(8,128)S(1)} collective-permute-done((f32[128,512]{1,0:T(8,128)S(1)}, f32[128,512]{1,0:T(8,128)S(1)}, u32[]{:S(2)}, u32[]{:S(2)}) %collective-permute-start.19) | collective-permute-done | bytes 262176 | tf_op jit(solution)/shard_map/ppermute | solution.py:42
  155.2 5.7 %collective-permute-done.21 = bf16[64,512]{1,0:T(8,128)(2,1)S(1)} collective-permute-done((bf16[64,512]{1,0:T(8,128)(2,1)S(1)}, bf16[64,512]{1,0:T(8,128)(2,1)S(1)}, u32[]{:S(2)}, u32[]{:S(2)}) %collective-permute-start.21) | collective-permute-done | bytes 65568 | tf_op jit(solution)/shard_map/ppermute | solution.py:56
  (52 shorter events, 29.2 us)
Async XLA Ops:
  0.0 20.8 %copy-start = (bf16[512,512]{1,0:T(8,128)(2,1)S(1)}, bf16[512,512]{1,0:T(8,128)(2,1)}, u32[]{:S(2)}) copy-start(bf16[512,512]{1,0:T(8,128)(2,1)} %param.2) | copy-start | bytes 1572868
  1.1 11.4 %collective-permute-start = (bf16[128,1024]{1,0:T(8,128)(2,1)S(1)}, bf16[128,1024]{1,0:T(8,128)(2,1)S(1)}, u32[]{:S(2)}, u32[]{:S(2)}) collective-permute-start(bf16[128,1024]{1,0:T(8,128)(2,1)S(1)} %get-tuple-element.12), channel_id=1, source_target_pairs={{0,4},{4,0},{1,5},{5,1},{2,6},{6,2},{3,7},{7,3},{8,12},{12,8},{9,1... | collective-permute-start | bytes 786440 | tf_op jit(solution)/shard_map/ppermute | solution.py:56
  6.1 12.5 %collective-permute-start.5 = (bf16[128,1024]{1,0:T(8,128)(2,1)S(1)}, bf16[128,1024]{1,0:T(8,128)(2,1)S(1)}, u32[]{:S(2)}, u32[]{:S(2)}) collective-permute-start(bf16[128,1024]{1,0:T(8,128)(2,1)S(1)} %get-tuple-element.11), channel_id=1, source_target_pairs={{0,8},{1,57},{8,0},{9,17},{16,24},{17,9},{24,16},{25,33},{32,40},{... | collective-permute-start | bytes 786440 | tf_op jit(solution)/shard_map/ppermute | solution.py:42
  12.6 13.4 %collective-permute-start.1 = (bf16[512,512]{1,0:T(8,128)(2,1)}, bf16[512,512]{1,0:T(8,128)(2,1)S(1)}, u32[]{:S(2)}, u32[]{:S(2)}) collective-permute-start(bf16[512,512]{1,0:T(8,128)(2,1)} %param.2), channel_id=1, source_target_pairs={{0,2},{1,7},{2,0},{3,5},{4,6},{5,3},{6,4},{7,1},{8,10},{9,15},{10,... | collective-permute-start | bytes 1572872 | tf_op jit(solution)/shard_map/ppermute | solution.py:42
  16.0 9.9 %collective-permute-start.6 = (bf16[128,1024]{1,0:T(8,128)(2,1)S(1)}, bf16[128,1024]{1,0:T(8,128)(2,1)S(1)}, u32[]{:S(2)}, u32[]{:S(2)}) collective-permute-start(bf16[128,1024]{1,0:T(8,128)(2,1)S(1)} %collective-permute-done), channel_id=1, source_target_pairs={{0,8},{1,57},{8,0},{9,17},{16,24},{17,9},{24,16},{25,33},{32,40},{... | collective-permute-start | bytes 786440 | tf_op jit(solution)/shard_map/ppermute | solution.py:42
  18.6 14.4 %collective-permute-start.7 = (bf16[256,1024]{1,0:T(8,128)(2,1)S(1)}, bf16[256,1024]{1,0:T(8,128)(2,1)S(1)}, u32[]{:S(2)}, u32[]{:S(2)}) collective-permute-start(bf16[256,1024]{1,0:T(8,128)(2,1)S(1)} %pad_maximum_fusion.1.first), channel_id=1, source_target_pairs={{0,56},{1,9},{8,16},{9,1},{16,8},{17,25},{24,32},{25,17},{32,24},{... | collective-permute-start | bytes 1572872 | tf_op jit(solution)/shard_map/ppermute | solution.py:42
  26.0 22.5 %collective-permute-start.2 = (bf16[1024,512]{1,0:T(8,128)(2,1)S(1)}, bf16[1024,512]{1,0:T(8,128)(2,1)S(1)}, u32[]{:S(2)}, u32[]{:S(2)}) collective-permute-start(bf16[1024,512]{1,0:T(8,128)(2,1)S(1)} %constant_dynamic-update-slice_fusion.own), channel_id=1, source_target_pairs={{0,6},{1,3},{2,4},{3,1},{4,2},{5,7},{6,0},{7,5},{8,14},{9,11},{10,... | collective-permute-start | bytes 3145736 | tf_op jit(solution)/shard_map/ppermute | solution.py:42
  31.1 13.4 %collective-permute-start.8 = (bf16[256,1024]{1,0:T(8,128)(2,1)S(1)}, bf16[256,1024]{1,0:T(8,128)(2,1)S(1)}, u32[]{:S(2)}, u32[]{:S(2)}) collective-permute-start(bf16[256,1024]{1,0:T(8,128)(2,1)S(1)} %constant_dynamic-update-slice_fusion.2.first_2), channel_id=1, source_target_pairs={{0,56},{1,9},{8,16},{9,1},{16,8},{17,25},{24,32},{25,17},{32,24},{... | collective-permute-start | bytes 1572872 | tf_op jit(solution)/shard_map/ppermute | solution.py:42
  44.6 19.0 %collective-permute-start.9 = (bf16[512,1024]{1,0:T(8,128)(2,1)S(1)}, bf16[512,1024]{1,0:T(8,128)(2,1)S(1)}, u32[]{:S(2)}, u32[]{:S(2)}) collective-permute-start(bf16[512,1024]{1,0:T(8,128)(2,1)S(1)} %pad_maximum_fusion), channel_id=1, source_target_pairs={{0,8},{1,57},{8,0},{9,17},{16,24},{17,9},{24,16},{25,33},{32,40},{... | collective-permute-start | bytes 3145736 | tf_op jit(solution)/shard_map/ppermute | solution.py:42
  46.6 24.2 %collective-permute-start.3 = (bf16[1024,512]{1,0:T(8,128)(2,1)S(1)}, bf16[1024,512]{1,0:T(8,128)(2,1)S(1)}, u32[]{:S(2)}, u32[]{:S(2)}) collective-permute-start(bf16[1024,512]{1,0:T(8,128)(2,1)S(1)} %constant_dynamic-update-slice_fusion.own), channel_id=1, source_target_pairs={{0,1},{1,0},{2,3},{3,2},{4,5},{5,4},{6,7},{7,6},{8,9},{9,8},{10,11... | collective-permute-start | bytes 3145736 | tf_op jit(solution)/shard_map/ppermute | solution.py:46
  48.5 22.3 %collective-permute-start.4 = (bf16[1024,512]{1,0:T(8,128)(2,1)S(1)}, bf16[1024,512]{1,0:T(8,128)(2,1)S(1)}, u32[]{:S(2)}, u32[]{:S(2)}) collective-permute-start(bf16[1024,512]{1,0:T(8,128)(2,1)S(1)} %collective-permute-done.2.far), channel_id=1, source_target_pairs={{0,1},{1,0},{2,3},{3,2},{4,5},{5,4},{6,7},{7,6},{8,9},{9,8},{10,11... | collective-permute-start | bytes 3145736 | tf_op jit(solution)/shard_map/ppermute | solution.py:46
  63.7 12.3 %collective-permute-start.10 = (bf16[512,512]{1,0:T(8,128)(2,1)S(1)}, bf16[512,512]{1,0:T(8,128)(2,1)S(1)}, u32[]{:S(2)}, u32[]{:S(2)}) collective-permute-start(bf16[512,512]{1,0:T(8,128)(2,1)S(1)} %get-tuple-element.10), channel_id=1, source_target_pairs={{0,56},{1,9},{8,16},{9,1},{16,8},{17,25},{24,32},{25,17},{32,24},{... | collective-permute-start | bytes 1572872 | tf_op jit(solution)/shard_map/ppermute | solution.py:42
  65.6 21.6 %collective-permute-start.15 = (bf16[512,512]{1,0:T(8,128)(2,1)S(1)}, bf16[512,512]{1,0:T(8,128)(2,1)S(1)}, u32[]{:S(2)}, u32[]{:S(2)}) collective-permute-start(bf16[512,512]{1,0:T(8,128)(2,1)S(1)} %get-tuple-element.9), channel_id=1, source_target_pairs={{0,56},{1,9},{8,16},{9,1},{16,8},{17,25},{24,32},{25,17},{32,24},{... | collective-permute-start | bytes 1572872 | tf_op jit(solution)/shard_map/ppermute | solution.py:42
  76.3 23.3 %collective-permute-start.11 = (f32[256,512]{1,0:T(8,128)S(1)}, f32[256,512]{1,0:T(8,128)S(1)}, u32[]{:S(2)}, u32[]{:S(2)}) collective-permute-start(f32[256,512]{1,0:T(8,128)S(1)} %last.5), channel_id=1, source_target_pairs={{0,448},{1,65},{64,128},{65,1},{128,64},{129,193},{192,256},{193,1... | collective-permute-start | bytes 1572872 | tf_op jit(solution)/shard_map/ppermute | solution.py:42
  87.6 23.3 %collective-permute-start.16 = (f32[256,512]{1,0:T(8,128)S(1)}, f32[256,512]{1,0:T(8,128)S(1)}, u32[]{:S(2)}, u32[]{:S(2)}) collective-permute-start(f32[256,512]{1,0:T(8,128)S(1)} %last.7), channel_id=1, source_target_pairs={{0,448},{1,65},{64,128},{65,1},{128,64},{129,193},{192,256},{193,1... | collective-permute-start | bytes 1572872 | tf_op jit(solution)/shard_map/ppermute | solution.py:42
  99.7 15.7 %collective-permute-start.12 = (f32[256,512]{1,0:T(8,128)S(1)}, f32[256,512]{1,0:T(8,128)S(1)}, u32[]{:S(2)}, u32[]{:S(2)}) collective-permute-start(f32[256,512]{1,0:T(8,128)S(1)} %slice_add_fusion.3), channel_id=1, source_target_pairs={{0,64},{1,449},{64,0},{65,129},{128,192},{129,65},{192,128},{193,2... | collective-permute-start | bytes 1572872 | tf_op jit(solution)/shard_map/ppermute | solution.py:42
  110.9 16.4 %collective-permute-start.17 = (f32[256,512]{1,0:T(8,128)S(1)}, f32[256,512]{1,0:T(8,128)S(1)}, u32[]{:S(2)}, u32[]{:S(2)}) collective-permute-start(f32[256,512]{1,0:T(8,128)S(1)} %slice_add_fusion), channel_id=1, source_target_pairs={{0,64},{1,449},{64,0},{65,129},{128,192},{129,65},{192,128},{193,2... | collective-permute-start | bytes 1572872 | tf_op jit(solution)/shard_map/ppermute | solution.py:42
  116.3 17.4 %collective-permute-start.13 = (f32[256,512]{1,0:T(8,128)}, f32[256,512]{1,0:T(8,128)}, u32[]{:S(2)}, u32[]{:S(2)}) collective-permute-start(f32[256,512]{1,0:T(8,128)} %slice_add_fusion.4), channel_id=1, source_target_pairs={{0,448},{1,65},{64,128},{65,1},{128,64},{129,193},{192,256},{193,1... | collective-permute-start | bytes 1572872 | tf_op jit(solution)/shard_map/ppermute | solution.py:42
  128.3 15.5 %collective-permute-start.18 = (f32[256,512]{1,0:T(8,128)}, f32[256,512]{1,0:T(8,128)}, u32[]{:S(2)}, u32[]{:S(2)}) collective-permute-start(f32[256,512]{1,0:T(8,128)} %slice_add_fusion.1), channel_id=1, source_target_pairs={{0,448},{1,65},{64,128},{65,1},{128,64},{129,193},{192,256},{193,1... | collective-permute-start | bytes 1572872 | tf_op jit(solution)/shard_map/ppermute | solution.py:42
  134.9 11.9 %collective-permute-start.14 = (f32[128,512]{1,0:T(8,128)S(1)}, f32[128,512]{1,0:T(8,128)S(1)}, u32[]{:S(2)}, u32[]{:S(2)}) collective-permute-start(f32[128,512]{1,0:T(8,128)S(1)} %slice.69), channel_id=1, source_target_pairs={{0,64},{1,449},{64,0},{65,129},{128,192},{129,65},{192,128},{193,2... | collective-permute-start | bytes 786440 | tf_op jit(solution)/shard_map/ppermute | solution.py:42
  144.9 8.3 %collective-permute-start.19 = (f32[128,512]{1,0:T(8,128)S(1)}, f32[128,512]{1,0:T(8,128)S(1)}, u32[]{:S(2)}, u32[]{:S(2)}) collective-permute-start(f32[128,512]{1,0:T(8,128)S(1)} %slice.76), channel_id=1, source_target_pairs={{0,64},{1,449},{64,0},{65,129},{128,192},{129,65},{192,128},{193,2... | collective-permute-start | bytes 786440 | tf_op jit(solution)/shard_map/ppermute | solution.py:42
  146.9 8.3 %collective-permute-start.20 = (bf16[64,512]{1,0:T(8,128)(2,1)S(1)}, bf16[64,512]{1,0:T(8,128)(2,1)S(1)}, u32[]{:S(2)}, u32[]{:S(2)}) collective-permute-start(bf16[64,512]{1,0:T(8,128)(2,1)S(1)} %get-tuple-element.16), channel_id=1, source_target_pairs={{0,4},{4,0},{1,5},{5,1},{2,6},{6,2},{3,7},{7,3},{8,12},{12,8},{9,1... | collective-permute-start | bytes 196616 | tf_op jit(solution)/shard_map/ppermute | solution.py:56
  153.3 7.7 %collective-permute-start.21 = (bf16[64,512]{1,0:T(8,128)(2,1)S(1)}, bf16[64,512]{1,0:T(8,128)(2,1)S(1)}, u32[]{:S(2)}, u32[]{:S(2)}) collective-permute-start(bf16[64,512]{1,0:T(8,128)(2,1)S(1)} %get-tuple-element.18), channel_id=1, source_target_pairs={{0,4},{4,0},{1,5},{5,1},{2,6},{6,2},{3,7},{7,3},{8,12},{12,8},{9,1... | collective-permute-start | bytes 196616 | tf_op jit(solution)/shard_map/ppermute | solution.py:56

commit v2 on v1

--- a/solution.py
+++ b/solution.py
@@ -17,6 +17,8 @@
 X = ("row_1", "col_0")
 Y = ("row_0",)
 Z = ("layer",)
+EXTRA = 16
+STRETCH = 2.3
 PLACES_Y = (0, 1, 4, 5, 7, 6, 3, 2)
 
 
@@ -140,27 +142,78 @@
     )(resident(left), *[resident(right) for right in rights])
 
 
-def last_kernel(first, count, side, total, left, right, out):
+def coded(value, out):
+    rows = value.shape[0]
+    square = jnp.sum(jnp.sum(value * value, axis=0, keepdims=True), axis=1, keepdims=True) / value.size
+    power = jnp.clip(jnp.floor(0.5 * jnp.log2(jnp.maximum(square, 1e-37))) - 1.0, -100.0, 100.0)
+    unit = jnp.abs(value) * jnp.exp2(-power)
+    grown = jnp.exp2(STRETCH * jnp.log2(unit + jnp.sqrt(unit * unit + 1.0)) - 14.0)
+    out[:rows, :] = jnp.where(value < 0.0, -grown, grown)
+    out[rows:, :] = jnp.broadcast_to(power, (EXTRA, out.shape[1]))
+
+
+def decoded(value):
+    rows = value.shape[0] - EXTRA
+    code = value[:rows, :]
+    grown = jnp.exp2((jnp.log2(jnp.abs(code)) + 14.0) * (1.0 / STRETCH))
+    unit = 0.5 * (grown - 1.0 / grown) * jnp.exp2(value[rows:rows + 1, :])
+    return jnp.where(code < 0.0, -unit, unit)
+
+
+def part_of(total, left, right, part, side):
     rows = total.shape[0] // 4
-    depth = right.shape[0]
-    for part in range(count):
-        at = pl.ds((first + part) * rows, rows)
-        width = right.shape[1]
-        out[part * rows:(part + 1) * rows, :] = total[at, side * width:(side + 1) * width] + jnp.dot(left[at, 3 * depth:], right[...], preferred_element_type=jnp.float32)
-
-
-def last(total, left, right, first, count, side):
-    rows = total.shape[0]
     depth, width = right.shape
-    return pl.pallas_call(
-        functools.partial(last_kernel, first, count, side),
-        out_shape=pltpu.VMEM((rows // 4 * count, width), jnp.float32),
+    at = pl.ds(part * rows, rows)
+    return total[at, side * width:(side + 1) * width] + jnp.dot(left[at, 3 * depth:], right[...], preferred_element_type=jnp.float32)
+
+
+def away_kernel(side, total, left, right, out):
+    coded(part_of(total, left, right, 0, side), out)
+
+
+def rest_kernel(side, total, left, right, out):
+    rows = total.shape[0] // 4
+    for part in range(3):
+        out[part * rows:(part + 1) * rows, :] = part_of(total, left, right, part + 1, side)
+
+
+def last(kernel, rows, total, left, right, side):
+    depth, width = right.shape
+    flops = 2 * sum(rows) * depth * width
+    return pl.pallas_call(
+        functools.partial(kernel, side),
+        out_shape=[pltpu.VMEM((count, width), jnp.float32) for count in rows],
         in_specs=[IN_VMEM] * 3,
+        out_specs=[IN_VMEM] * len(rows),
+        cost_estimate=pl.CostEstimate(flops=flops, transcendentals=0, bytes_accessed=8 * sum(rows) * width),
+        compiler_params=pltpu.CompilerParams(vmem_limit_bytes=16 << 20),
+    )(resident(total), resident(left), resident(right))
+
+
+def more_kernel(first, base, value, out):
+    rows = value.shape[0] - EXTRA
+    total = base[first:first + rows, :] + decoded(value)
+    if out.shape[0] > rows:
+        coded(total, out)
+    else:
+        out[...] = total
+
+
+def more(base, first, value, extra):
+    rows, width = value.shape
+    return pl.pallas_call(
+        functools.partial(more_kernel, first),
+        out_shape=pltpu.VMEM((rows - EXTRA + extra, width), jnp.float32),
+        in_specs=[IN_VMEM] * 2,
         out_specs=IN_VMEM,
-        cost_estimate=pl.CostEstimate(flops=rows // 2 * count * depth * width, transcendentals=0, bytes_accessed=2 * count * rows * width),
-        compiler_params=pltpu.CompilerParams(vmem_limit_bytes=16 << 20),
-        name="last",
-    )(resident(total), resident(left), resident(right))
+        cost_estimate=pl.CostEstimate(flops=20 * value.size, transcendentals=4 * value.size, bytes_accessed=12 * value.size),
+        compiler_params=pltpu.CompilerParams(vmem_limit_bytes=8 << 20),
+        name="more",
+    )(resident(base), resident(value.astype(jnp.float32)))
+
+
+def sent(value, onward):
+    return exchange(value.astype(jnp.float16), Z, onward)
 
 
 def step(left_matrix, right_matrix):
@@ -190,21 +243,19 @@
     left = ordered(left_own, left_far, own_theirs, far_theirs)
     total = most(left, (first, first_2, second, second_2, third))
     kept = []
-    out_came = []
     for side, columns in enumerate((fourth, fourth_right)):
-        away = last(total, left, columns, 0, 1, side)
-        rest = last(total, left, columns, 1, 3, side)
-        rows = away.shape[0]
-        far, close, own = rest[:rows], rest[rows:2 * rows], rest[2 * rows:]
-        far = far + exchange(away, Z, False)
-        close = close + exchange(far, Z, True)
-        own = own + exchange(close, Z, False)
+        rows = total.shape[0] // 4
+        away, = last(away_kernel, (rows + EXTRA,), total, left, columns, side)
+        rest, = last(rest_kernel, (3 * rows,), total, left, columns, side)
+        far = more(rest, 0, sent(away, False), EXTRA)
+        close = more(rest, rows, sent(far, True), EXTRA)
+        own = more(rest, 2 * rows, sent(close, False), 0)
         own = (own[:rows // 2] + exchange(own[rows // 2:], Z, True)).astype(jnp.bfloat16)
-        kept.append(own[:rows // 4])
-        out_came.append(swap_high(own[rows // 4:]))
-    kept = jnp.concatenate(kept, axis=1)
-    out_came = jnp.concatenate(out_came, axis=1)
-    return jnp.concatenate([jnp.where(high == 0, kept, out_came), jnp.where(high == 0, out_came, kept)], axis=1)
+        kept.append(own)
+    whole = jnp.concatenate(kept, axis=1)
+    out_came = swap_high(whole[rows // 4:])
+    whole = whole[:rows // 4]
+    return jnp.concatenate([jnp.where(high == 0, whole, out_came), jnp.where(high == 0, out_came, whole)], axis=1)
 
 
 def solution(mesh):

time: 163 us -> 143 us (0.88)
  waiting for transfers between devices: 72.7 us -> 55.5 us
  Pallas kernels: 6.9 us -> 12.8 us
  starting transfers between devices: 75.2 us -> 70.4 us
  other arithmetic: 5.12 us -> 1.55 us
    ppermute x17, waiting for transfers between devices: 63 us -> 45.1 us  [exchange(): return lax.ppermute(value, (*axes, CORE), pairs)]
    pallas_call x4 -> x10, Pallas kernels: 1.74 us -> 7.59 us  [the longest x6 4.64 us: more(): pl.pallas_call(functools.partial(more_kernel, first), out_shape=pltpu.VME...]
    add x6 -> x0, other arithmetic: 4.17 us -> none  [the longest x2 2.24 us: step(): own = own + exchange(close, Z, False)]
    ppermute x17, starting transfers between devices: 62.1 us -> 59.2 us  [exchange(): return lax.ppermute(value, (*axes, CORE), pairs)]
    ppermute x3 -> x2, starting transfers between devices: 8.77 us -> 6.85 us  [swap_high(): return lax.ppermute(value, ('row_1',), [(0, 1), (1, 0)])]
    ppermute x3 -> x2, waiting for transfers between devices: 9.62 us -> 10.3 us  [swap_high(): return lax.ppermute(value, ('row_1',), [(0, 1), (1, 0)])]
  transfers between devices with their start and end apart: 22 -> 21, of which waited for: 11 -> 12; matrix products, arithmetic and copies ran while one was open for 3% -> 1% of each run, Pallas kernels for 4% -> 9%
where the time goes in v2:
time: 143 us; the launch traced here: 142 us
  starting transfers between devices  70.4 us (49%)
  waiting for transfers between devices  55.5 us (39%)
  Pallas kernels  12.8 us (9%)
  other arithmetic  1.55 us (1%)
    ppermute x17, starting transfers between devices, exchange(): return lax.ppermute(value, (*axes, CORE), pairs)  59.2 us
    ppermute x17, waiting for transfers between devices, exchange(): return lax.ppermute(value, (*axes, CORE), pairs)  45.1 us
    ppermute x2, waiting for transfers between devices, swap_high(): return lax.ppermute(value, ('row_1',), [(0, 1), (1, 0)])  10.3 us
    ppermute x2, starting transfers between devices, swap_high(): return lax.ppermute(value, ('row_1',), [(0, 1), (1, 0)])  6.85 us
    pallas_call x6, Pallas kernels, more(): pl.pallas_call(functools.partial(more_kernel, first), out_shape=pltpu.VME...  4.64 us
    ppermute x2, starting transfers between devices, swap_cores(): return lax.ppermute(value, (CORE,), [(0, 1), (1, 0)])  4.33 us
    pallas_call x1, Pallas kernels, most(): pl.pallas_call(most_kernel, out_shape=pltpu.VMEM((rows, width), jnp.float...  3.41 us
    pallas_call x4, Pallas kernels, last(): pl.pallas_call(functools.partial(kernel, side), out_shape=[pltpu.VMEM((co...  2.95 us
  transfers between devices with their start and end apart: 21, of which 12 were waited for; matrix products, arithmetic and copies ran while one was open for 1% of the time, Pallas kernels for 9%

profile of v2, /device:TPU:32, one launch (start us, length us, event | category | flops | bytes accessed | tf_op | source)
XLA Modules:
  0.0 142.0 jit_solution(7292425477399994013)
XLA Ops:
  1.1 4.9 %collective-permute-start = (bf16[128,1024]{1,0:T(8,128)(2,1)S(1)}, bf16[128,1024]{1,0:T(8,128)(2,1)S(1)}, u32[]{:S(2)}, u32[]{:S(2)}) collective-permute-start(bf16[128,1024]{1,0:T(8,128)(2,1)S(1)} %get-tuple-element.12), channel_id=1, source_target_pairs={{0,4},{4,0},{1,5},{5,1},{2,6},{6,2},{3,7},{7,3},{8,12},{12,8},{9,1... | collective-permute-start | bytes 786440 | tf_op jit(solution)/shard_map/ppermute | solution.py:58
  6.1 2.6 %collective-permute-start.5 = (bf16[128,1024]{1,0:T(8,128)(2,1)S(1)}, bf16[128,1024]{1,0:T(8,128)(2,1)S(1)}, u32[]{:S(2)}, u32[]{:S(2)}) collective-permute-start(bf16[128,1024]{1,0:T(8,128)(2,1)S(1)} %get-tuple-element.11), channel_id=1, source_target_pairs={{0,8},{1,57},{8,0},{9,17},{16,24},{17,9},{24,16},{25,33},{32,40},{... | collective-permute-start | bytes 786440 | tf_op jit(solution)/shard_map/ppermute | solution.py:44
  8.7 3.9 %collective-permute-done = bf16[128,1024]{1,0:T(8,128)(2,1)S(1)} collective-permute-done((bf16[128,1024]{1,0:T(8,128)(2,1)S(1)}, bf16[128,1024]{1,0:T(8,128)(2,1)S(1)}, u32[]{:S(2)}, u32[]{:S(2)}) %collective-permute-start) | collective-permute-done | bytes 262176 | tf_op jit(solution)/shard_map/ppermute | solution.py:58
  12.6 3.4 %collective-permute-start.1 = (bf16[512,512]{1,0:T(8,128)(2,1)}, bf16[512,512]{1,0:T(8,128)(2,1)S(1)}, u32[]{:S(2)}, u32[]{:S(2)}) collective-permute-start(bf16[512,512]{1,0:T(8,128)(2,1)} %param.2), channel_id=1, source_target_pairs={{0,2},{1,7},{2,0},{3,5},{4,6},{5,3},{6,4},{7,1},{8,10},{9,15},{10,... | collective-permute-start | bytes 1572872 | tf_op jit(solution)/shard_map/ppermute | solution.py:44
  16.0 2.6 %collective-permute-start.6 = (bf16[128,1024]{1,0:T(8,128)(2,1)S(1)}, bf16[128,1024]{1,0:T(8,128)(2,1)S(1)}, u32[]{:S(2)}, u32[]{:S(2)}) collective-permute-start(bf16[128,1024]{1,0:T(8,128)(2,1)S(1)} %collective-permute-done), channel_id=1, source_target_pairs={{0,8},{1,57},{8,0},{9,17},{16,24},{17,9},{24,16},{25,33},{32,40},{... | collective-permute-start | bytes 786440 | tf_op jit(solution)/shard_map/ppermute | solution.py:44
  18.6 2.1 %collective-permute-start.7 = (bf16[256,1024]{1,0:T(8,128)(2,1)S(1)}, bf16[256,1024]{1,0:T(8,128)(2,1)S(1)}, u32[]{:S(2)}, u32[]{:S(2)}) collective-permute-start(bf16[256,1024]{1,0:T(8,128)(2,1)S(1)} %pad_maximum_fusion.1.first), channel_id=1, source_target_pairs={{0,56},{1,9},{8,16},{9,1},{16,8},{17,25},{24,32},{25,17},{32,24},{... | collective-permute-start | bytes 1572872 | tf_op jit(solution)/shard_map/ppermute | solution.py:44
  20.8 5.1 %collective-permute-done.6 = bf16[128,1024]{1,0:T(8,128)(2,1)S(1)} collective-permute-done((bf16[128,1024]{1,0:T(8,128)(2,1)S(1)}, bf16[128,1024]{1,0:T(8,128)(2,1)S(1)}, u32[]{:S(2)}, u32[]{:S(2)}) %collective-permute-start.6) | collective-permute-done | bytes 262176 | tf_op jit(solution)/shard_map/ppermute | solution.py:44
  26.0 5.1 %collective-permute-start.2 = (bf16[1024,512]{1,0:T(8,128)(2,1)S(1)}, bf16[1024,512]{1,0:T(8,128)(2,1)S(1)}, u32[]{:S(2)}, u32[]{:S(2)}) collective-permute-start(bf16[1024,512]{1,0:T(8,128)(2,1)S(1)} %constant_dynamic-update-slice_fusion.own), channel_id=1, source_target_pairs={{0,6},{1,3},{2,4},{3,1},{4,2},{5,7},{6,0},{7,5},{8,14},{9,11},{10,... | collective-permute-start | bytes 3145736 | tf_op jit(solution)/shard_map/ppermute | solution.py:44
  33.1 11.5 %collective-permute-done.8.second_2 = bf16[256,1024]{1,0:T(8,128)(2,1)S(1)} collective-permute-done((bf16[256,1024]{1,0:T(8,128)(2,1)S(1)}, bf16[256,1024]{1,0:T(8,128)(2,1)S(1)}, u32[]{:S(2)}, u32[]{:S(2)}) %collective-permute-start.8) | collective-permute-done | bytes 524320 | tf_op jit(solution)/shard_map/ppermute | solution.py:44
  44.6 1.9 %collective-permute-start.9 = (bf16[512,1024]{1,0:T(8,128)(2,1)S(1)}, bf16[512,1024]{1,0:T(8,128)(2,1)S(1)}, u32[]{:S(2)}, u32[]{:S(2)}) collective-permute-start(bf16[512,1024]{1,0:T(8,128)(2,1)S(1)} %pad_maximum_fusion), channel_id=1, source_target_pairs={{0,8},{1,57},{8,0},{9,17},{16,24},{17,9},{24,16},{25,33},{32,40},{... | collective-permute-start | bytes 3145736 | tf_op jit(solution)/shard_map/ppermute | solution.py:44
  48.5 2.4 %collective-permute-start.4 = (bf16[1024,512]{1,0:T(8,128)(2,1)S(1)}, bf16[1024,512]{1,0:T(8,128)(2,1)S(1)}, u32[]{:S(2)}, u32[]{:S(2)}) collective-permute-start(bf16[1024,512]{1,0:T(8,128)(2,1)S(1)} %collective-permute-done.2.far), channel_id=1, source_target_pairs={{0,1},{1,0},{2,3},{3,2},{4,5},{5,4},{6,7},{7,6},{8,9},{9,8},{10,11... | collective-permute-start | bytes 3145736 | tf_op jit(solution)/shard_map/ppermute | solution.py:48
  50.9 12.7 %collective-permute-done.9.third = bf16[512,1024]{1,0:T(8,128)(2,1)S(1)} collective-permute-done((bf16[512,1024]{1,0:T(8,128)(2,1)S(1)}, bf16[512,1024]{1,0:T(8,128)(2,1)S(1)}, u32[]{:S(2)}, u32[]{:S(2)}) %collective-permute-start.9) | collective-permute-done | bytes 1048608 | tf_op jit(solution)/shard_map/ppermute | solution.py:44
  65.6 5.1 %collective-permute-start.15 = (bf16[512,512]{1,0:T(8,128)(2,1)S(1)}, bf16[512,512]{1,0:T(8,128)(2,1)S(1)}, u32[]{:S(2)}, u32[]{:S(2)}) collective-permute-start(bf16[512,512]{1,0:T(8,128)(2,1)S(1)} %get-tuple-element.10), channel_id=1, source_target_pairs={{0,56},{1,9},{8,16},{9,1},{16,8},{17,25},{24,32},{25,17},{32,24},{... | collective-permute-start | bytes 1572872 | tf_op jit(solution)/shard_map/ppermute | solution.py:44
  72.6 3.4 %most.1.total = f32[1024,1024]{1,0:T(8,128)S(1)} custom-call(bf16[1024,2048]{1,0:T(8,128)(2,1)S(1)} %order_left.1.left, bf16[256,1024]{1,0:T(8,128)(2,1)S(1)} %pad_maximum_fusion.1.first, bf16[256,1024]{1,0:T(8,128)(2,1)S(1)} %constant_dynamic-update-slice_fusion.2.first_2, bf16[256,1024]{1,0:T(8,128)(2,1)S(1)} %collective-permute-done.7.second, ...), custom_call_target="tpu_custom_call" | custom-call | flops 3221225472 | bytes 4194304 | tf_op jit(solution)/shard_map/most/pallas_call | solution.py:134
  76.9 10.9 %collective-permute-start.11 = (f16[272,512]{1,0:T(8,128)(2,1)S(1)}, f16[272,512]{1,0:T(8,128)(2,1)S(1)}, u32[]{:S(2)}, u32[]{:S(2)}) collective-permute-start(f16[272,512]{1,0:T(8,128)(2,1)S(1)} %convert_element_type.42), channel_id=1, source_target_pairs={{0,448},{1,65},{64,128},{65,1},{128,64},{129,193},{192,256},{193,1... | collective-permute-start | bytes 835592 | tf_op jit(solution)/shard_map/ppermute | solution.py:44
  88.9 4.6 %collective-permute-start.16 = (f16[272,512]{1,0:T(8,128)(2,1)S(1)}, f16[272,512]{1,0:T(8,128)(2,1)S(1)}, u32[]{:S(2)}, u32[]{:S(2)}) collective-permute-start(f16[272,512]{1,0:T(8,128)(2,1)S(1)} %convert_element_type.49), channel_id=1, source_target_pairs={{0,448},{1,65},{64,128},{65,1},{128,64},{129,193},{192,256},{193,1... | collective-permute-start | bytes 835592 | tf_op jit(solution)/shard_map/ppermute | solution.py:44
  99.0 2.4 %collective-permute-done.16 = f16[272,512]{1,0:T(8,128)(2,1)S(1)} collective-permute-done((f16[272,512]{1,0:T(8,128)(2,1)S(1)}, f16[272,512]{1,0:T(8,128)(2,1)S(1)}, u32[]{:S(2)}, u32[]{:S(2)}) %collective-permute-start.16) | collective-permute-done | bytes 278560 | tf_op jit(solution)/shard_map/ppermute | solution.py:44
  102.5 2.1 %collective-permute-start.17 = (f16[272,512]{1,0:T(8,128)(2,1)S(1)}, f16[272,512]{1,0:T(8,128)(2,1)S(1)}, u32[]{:S(2)}, u32[]{:S(2)}) collective-permute-start(f16[272,512]{1,0:T(8,128)(2,1)S(1)} %convert_element_type.51), channel_id=1, source_target_pairs={{0,64},{1,449},{64,0},{65,129},{128,192},{129,65},{192,128},{193,2... | collective-permute-start | bytes 835592 | tf_op jit(solution)/shard_map/ppermute | solution.py:44
  104.6 2.4 %collective-permute-done.12 = f16[272,512]{1,0:T(8,128)(2,1)S(1)} collective-permute-done((f16[272,512]{1,0:T(8,128)(2,1)S(1)}, f16[272,512]{1,0:T(8,128)(2,1)S(1)}, u32[]{:S(2)}, u32[]{:S(2)}) %collective-permute-start.12) | collective-permute-done | bytes 278560 | tf_op jit(solution)/shard_map/ppermute | solution.py:44
  108.1 4.6 %collective-permute-start.13 = (f16[272,512]{1,0:T(8,128)(2,1)S(1)}, f16[272,512]{1,0:T(8,128)(2,1)S(1)}, u32[]{:S(2)}, u32[]{:S(2)}) collective-permute-start(f16[272,512]{1,0:T(8,128)(2,1)S(1)} %convert_element_type.46), channel_id=1, source_target_pairs={{0,448},{1,65},{64,128},{65,1},{128,64},{129,193},{192,256},{193,1... | collective-permute-start | bytes 835592 | tf_op jit(solution)/shard_map/ppermute | solution.py:44
  114.2 4.4 %collective-permute-start.18 = (f16[272,512]{1,0:T(8,128)(2,1)S(1)}, f16[272,512]{1,0:T(8,128)(2,1)S(1)}, u32[]{:S(2)}, u32[]{:S(2)}) collective-permute-start(f16[272,512]{1,0:T(8,128)(2,1)S(1)} %convert_element_type.53), channel_id=1, source_target_pairs={{0,448},{1,65},{64,128},{65,1},{128,64},{129,193},{192,256},{193,1... | collective-permute-start | bytes 835592 | tf_op jit(solution)/shard_map/ppermute | solution.py:44
  121.0 3.2 %collective-permute-done.18 = f16[272,512]{1,0:T(8,128)(2,1)S(1)} collective-permute-done((f16[272,512]{1,0:T(8,128)(2,1)S(1)}, f16[272,512]{1,0:T(8,128)(2,1)S(1)}, u32[]{:S(2)}, u32[]{:S(2)}) %collective-permute-start.18) | collective-permute-done | bytes 278560 | tf_op jit(solution)/shard_map/ppermute | solution.py:44
  127.4 5.5 %collective-permute-done.19 = f32[128,512]{1,0:T(8,128)S(1)} collective-permute-done((f32[128,512]{1,0:T(8,128)S(1)}, f32[128,512]{1,0:T(8,128)S(1)}, u32[]{:S(2)}, u32[]{:S(2)}) %collective-permute-start.19) | collective-permute-done | bytes 262176 | tf_op jit(solution)/shard_map/ppermute | solution.py:44
  134.8 6.4 %collective-permute-done.20 = bf16[64,1024]{1,0:T(8,128)(2,1)S(1)} collective-permute-done((bf16[64,1024]{1,0:T(8,128)(2,1)S(1)}, bf16[64,1024]{1,0:T(8,128)(2,1)S(1)}, u32[]{:S(2)}, u32[]{:S(2)}) %collective-permute-start.20) | collective-permute-done | bytes 131104 | tf_op jit(solution)/shard_map/ppermute | solution.py:58
  (59 shorter events, 28.2 us)
Async XLA Ops:
  0.0 20.8 %copy-start = (bf16[512,512]{1,0:T(8,128)(2,1)S(1)}, bf16[512,512]{1,0:T(8,128)(2,1)}, u32[]{:S(2)}) copy-start(bf16[512,512]{1,0:T(8,128)(2,1)} %param.2) | copy-start | bytes 1572868
  1.1 11.4 %collective-permute-start = (bf16[128,1024]{1,0:T(8,128)(2,1)S(1)}, bf16[128,1024]{1,0:T(8,128)(2,1)S(1)}, u32[]{:S(2)}, u32[]{:S(2)}) collective-permute-start(bf16[128,1024]{1,0:T(8,128)(2,1)S(1)} %get-tuple-element.12), channel_id=1, source_target_pairs={{0,4},{4,0},{1,5},{5,1},{2,6},{6,2},{3,7},{7,3},{8,12},{12,8},{9,1... | collective-permute-start | bytes 786440 | tf_op jit(solution)/shard_map/ppermute | solution.py:58
  6.1 12.5 %collective-permute-start.5 = (bf16[128,1024]{1,0:T(8,128)(2,1)S(1)}, bf16[128,1024]{1,0:T(8,128)(2,1)S(1)}, u32[]{:S(2)}, u32[]{:S(2)}) collective-permute-start(bf16[128,1024]{1,0:T(8,128)(2,1)S(1)} %get-tuple-element.11), channel_id=1, source_target_pairs={{0,8},{1,57},{8,0},{9,17},{16,24},{17,9},{24,16},{25,33},{32,40},{... | collective-permute-start | bytes 786440 | tf_op jit(solution)/shard_map/ppermute | solution.py:44
  12.6 13.4 %collective-permute-start.1 = (bf16[512,512]{1,0:T(8,128)(2,1)}, bf16[512,512]{1,0:T(8,128)(2,1)S(1)}, u32[]{:S(2)}, u32[]{:S(2)}) collective-permute-start(bf16[512,512]{1,0:T(8,128)(2,1)} %param.2), channel_id=1, source_target_pairs={{0,2},{1,7},{2,0},{3,5},{4,6},{5,3},{6,4},{7,1},{8,10},{9,15},{10,... | collective-permute-start | bytes 1572872 | tf_op jit(solution)/shard_map/ppermute | solution.py:44
  16.0 9.9 %collective-permute-start.6 = (bf16[128,1024]{1,0:T(8,128)(2,1)S(1)}, bf16[128,1024]{1,0:T(8,128)(2,1)S(1)}, u32[]{:S(2)}, u32[]{:S(2)}) collective-permute-start(bf16[128,1024]{1,0:T(8,128)(2,1)S(1)} %collective-permute-done), channel_id=1, source_target_pairs={{0,8},{1,57},{8,0},{9,17},{16,24},{17,9},{24,16},{25,33},{32,40},{... | collective-permute-start | bytes 786440 | tf_op jit(solution)/shard_map/ppermute | solution.py:44
  18.6 14.4 %collective-permute-start.7 = (bf16[256,1024]{1,0:T(8,128)(2,1)S(1)}, bf16[256,1024]{1,0:T(8,128)(2,1)S(1)}, u32[]{:S(2)}, u32[]{:S(2)}) collective-permute-start(bf16[256,1024]{1,0:T(8,128)(2,1)S(1)} %pad_maximum_fusion.1.first), channel_id=1, source_target_pairs={{0,56},{1,9},{8,16},{9,1},{16,8},{17,25},{24,32},{25,17},{32,24},{... | collective-permute-start | bytes 1572872 | tf_op jit(solution)/shard_map/ppermute | solution.py:44
  26.0 22.5 %collective-permute-start.2 = (bf16[1024,512]{1,0:T(8,128)(2,1)S(1)}, bf16[1024,512]{1,0:T(8,128)(2,1)S(1)}, u32[]{:S(2)}, u32[]{:S(2)}) collective-permute-start(bf16[1024,512]{1,0:T(8,128)(2,1)S(1)} %constant_dynamic-update-slice_fusion.own), channel_id=1, source_target_pairs={{0,6},{1,3},{2,4},{3,1},{4,2},{5,7},{6,0},{7,5},{8,14},{9,11},{10,... | collective-permute-start | bytes 3145736 | tf_op jit(solution)/shard_map/ppermute | solution.py:44
  31.1 13.4 %collective-permute-start.8 = (bf16[256,1024]{1,0:T(8,128)(2,1)S(1)}, bf16[256,1024]{1,0:T(8,128)(2,1)S(1)}, u32[]{:S(2)}, u32[]{:S(2)}) collective-permute-start(bf16[256,1024]{1,0:T(8,128)(2,1)S(1)} %constant_dynamic-update-slice_fusion.2.first_2), channel_id=1, source_target_pairs={{0,56},{1,9},{8,16},{9,1},{16,8},{17,25},{24,32},{25,17},{32,24},{... | collective-permute-start | bytes 1572872 | tf_op jit(solution)/shard_map/ppermute | solution.py:44
  44.6 19.0 %collective-permute-start.9 = (bf16[512,1024]{1,0:T(8,128)(2,1)S(1)}, bf16[512,1024]{1,0:T(8,128)(2,1)S(1)}, u32[]{:S(2)}, u32[]{:S(2)}) collective-permute-start(bf16[512,1024]{1,0:T(8,128)(2,1)S(1)} %pad_maximum_fusion), channel_id=1, source_target_pairs={{0,8},{1,57},{8,0},{9,17},{16,24},{17,9},{24,16},{25,33},{32,40},{... | collective-permute-start | bytes 3145736 | tf_op jit(solution)/shard_map/ppermute | solution.py:44
  46.6 24.2 %collective-permute-start.3 = (bf16[1024,512]{1,0:T(8,128)(2,1)S(1)}, bf16[1024,512]{1,0:T(8,128)(2,1)S(1)}, u32[]{:S(2)}, u32[]{:S(2)}) collective-permute-start(bf16[1024,512]{1,0:T(8,128)(2,1)S(1)} %constant_dynamic-update-slice_fusion.own), channel_id=1, source_target_pairs={{0,1},{1,0},{2,3},{3,2},{4,5},{5,4},{6,7},{7,6},{8,9},{9,8},{10,11... | collective-permute-start | bytes 3145736 | tf_op jit(solution)/shard_map/ppermute | solution.py:48
  48.5 22.3 %collective-permute-start.4 = (bf16[1024,512]{1,0:T(8,128)(2,1)S(1)}, bf16[1024,512]{1,0:T(8,128)(2,1)S(1)}, u32[]{:S(2)}, u32[]{:S(2)}) collective-permute-start(bf16[1024,512]{1,0:T(8,128)(2,1)S(1)} %collective-permute-done.2.far), channel_id=1, source_target_pairs={{0,1},{1,0},{2,3},{3,2},{4,5},{5,4},{6,7},{7,6},{8,9},{9,8},{10,11... | collective-permute-start | bytes 3145736 | tf_op jit(solution)/shard_map/ppermute | solution.py:48
  63.7 12.3 %collective-permute-start.10 = (bf16[512,512]{1,0:T(8,128)(2,1)S(1)}, bf16[512,512]{1,0:T(8,128)(2,1)S(1)}, u32[]{:S(2)}, u32[]{:S(2)}) collective-permute-start(bf16[512,512]{1,0:T(8,128)(2,1)S(1)} %get-tuple-element.9), channel_id=1, source_target_pairs={{0,56},{1,9},{8,16},{9,1},{16,8},{17,25},{24,32},{25,17},{32,24},{... | collective-permute-start | bytes 1572872 | tf_op jit(solution)/shard_map/ppermute | solution.py:44
  65.6 22.3 %collective-permute-start.15 = (bf16[512,512]{1,0:T(8,128)(2,1)S(1)}, bf16[512,512]{1,0:T(8,128)(2,1)S(1)}, u32[]{:S(2)}, u32[]{:S(2)}) collective-permute-start(bf16[512,512]{1,0:T(8,128)(2,1)S(1)} %get-tuple-element.10), channel_id=1, source_target_pairs={{0,56},{1,9},{8,16},{9,1},{16,8},{17,25},{24,32},{25,17},{32,24},{... | collective-permute-start | bytes 1572872 | tf_op jit(solution)/shard_map/ppermute | solution.py:44
  76.9 18.4 %collective-permute-start.11 = (f16[272,512]{1,0:T(8,128)(2,1)S(1)}, f16[272,512]{1,0:T(8,128)(2,1)S(1)}, u32[]{:S(2)}, u32[]{:S(2)}) collective-permute-start(f16[272,512]{1,0:T(8,128)(2,1)S(1)} %convert_element_type.42), channel_id=1, source_target_pairs={{0,448},{1,65},{64,128},{65,1},{128,64},{129,193},{192,256},{193,1... | collective-permute-start | bytes 835592 | tf_op jit(solution)/shard_map/ppermute | solution.py:44
  88.9 12.5 %collective-permute-start.16 = (f16[272,512]{1,0:T(8,128)(2,1)S(1)}, f16[272,512]{1,0:T(8,128)(2,1)S(1)}, u32[]{:S(2)}, u32[]{:S(2)}) collective-permute-start(f16[272,512]{1,0:T(8,128)(2,1)S(1)} %convert_element_type.49), channel_id=1, source_target_pairs={{0,448},{1,65},{64,128},{65,1},{128,64},{129,193},{192,256},{193,1... | collective-permute-start | bytes 835592 | tf_op jit(solution)/shard_map/ppermute | solution.py:44
  96.5 10.5 %collective-permute-start.12 = (f16[272,512]{1,0:T(8,128)(2,1)S(1)}, f16[272,512]{1,0:T(8,128)(2,1)S(1)}, u32[]{:S(2)}, u32[]{:S(2)}) collective-permute-start(f16[272,512]{1,0:T(8,128)(2,1)S(1)} %convert_element_type.44), channel_id=1, source_target_pairs={{0,64},{1,449},{64,0},{65,129},{128,192},{129,65},{192,128},{193,2... | collective-permute-start | bytes 835592 | tf_op jit(solution)/shard_map/ppermute | solution.py:44
  102.5 10.6 %collective-permute-start.17 = (f16[272,512]{1,0:T(8,128)(2,1)S(1)}, f16[272,512]{1,0:T(8,128)(2,1)S(1)}, u32[]{:S(2)}, u32[]{:S(2)}) collective-permute-start(f16[272,512]{1,0:T(8,128)(2,1)S(1)} %convert_element_type.51), channel_id=1, source_target_pairs={{0,64},{1,449},{64,0},{65,129},{128,192},{129,65},{192,128},{193,2... | collective-permute-start | bytes 835592 | tf_op jit(solution)/shard_map/ppermute | solution.py:44
  108.1 10.6 %collective-permute-start.13 = (f16[272,512]{1,0:T(8,128)(2,1)S(1)}, f16[272,512]{1,0:T(8,128)(2,1)S(1)}, u32[]{:S(2)}, u32[]{:S(2)}) collective-permute-start(f16[272,512]{1,0:T(8,128)(2,1)S(1)} %convert_element_type.46), channel_id=1, source_target_pairs={{0,448},{1,65},{64,128},{65,1},{128,64},{129,193},{192,256},{193,1... | collective-permute-start | bytes 835592 | tf_op jit(solution)/shard_map/ppermute | solution.py:44
  114.2 10.0 %collective-permute-start.18 = (f16[272,512]{1,0:T(8,128)(2,1)S(1)}, f16[272,512]{1,0:T(8,128)(2,1)S(1)}, u32[]{:S(2)}, u32[]{:S(2)}) collective-permute-start(f16[272,512]{1,0:T(8,128)(2,1)S(1)} %convert_element_type.53), channel_id=1, source_target_pairs={{0,448},{1,65},{64,128},{65,1},{128,64},{129,193},{192,256},{193,1... | collective-permute-start | bytes 835592 | tf_op jit(solution)/shard_map/ppermute | solution.py:44
  119.1 8.3 %collective-permute-start.14 = (f32[128,512]{1,0:T(8,128)S(1)}, f32[128,512]{1,0:T(8,128)S(1)}, u32[]{:S(2)}, u32[]{:S(2)}) collective-permute-start(f32[128,512]{1,0:T(8,128)S(1)} %slice.34), channel_id=1, source_target_pairs={{0,64},{1,449},{64,0},{65,129},{128,192},{129,65},{192,128},{193,2... | collective-permute-start | bytes 786440 | tf_op jit(solution)/shard_map/ppermute | solution.py:44
  124.6 8.3 %collective-permute-start.19 = (f32[128,512]{1,0:T(8,128)S(1)}, f32[128,512]{1,0:T(8,128)S(1)}, u32[]{:S(2)}, u32[]{:S(2)}) collective-permute-start(f32[128,512]{1,0:T(8,128)S(1)} %slice.37), channel_id=1, source_target_pairs={{0,64},{1,449},{64,0},{65,129},{128,192},{129,65},{192,128},{193,2... | collective-permute-start | bytes 786440 | tf_op jit(solution)/shard_map/ppermute | solution.py:44
  132.9 8.4 %collective-permute-start.20 = (bf16[64,1024]{1,0:T(8,128)(2,1)S(1)}, bf16[64,1024]{1,0:T(8,128)(2,1)S(1)}, u32[]{:S(2)}, u32[]{:S(2)}) collective-permute-start(bf16[64,1024]{1,0:T(8,128)(2,1)S(1)} %pad_maximum_fusion.3), channel_id=1, source_target_pairs={{0,4},{4,0},{1,5},{5,1},{2,6},{6,2},{3,7},{7,3},{8,12},{12,8},{9,1... | collective-permute-start | bytes 393224 | tf_op jit(solution)/shard_map/ppermute | solution.py:58

commit v3 on v2

--- a/solution.py
+++ b/solution.py
@@ -142,46 +142,62 @@
     )(resident(left), *[resident(right) for right in rights])
 
 
-def coded(value, out):
-    rows = value.shape[0]
-    square = jnp.sum(jnp.sum(value * value, axis=0, keepdims=True), axis=1, keepdims=True) / value.size
-    power = jnp.clip(jnp.floor(0.5 * jnp.log2(jnp.maximum(square, 1e-37))) - 1.0, -100.0, 100.0)
-    unit = jnp.abs(value) * jnp.exp2(-power)
-    grown = jnp.exp2(STRETCH * jnp.log2(unit + jnp.sqrt(unit * unit + 1.0)) - 14.0)
-    out[:rows, :] = jnp.where(value < 0.0, -grown, grown)
+SLAB = 32
+
+
+def level(square, count):
+    square = jnp.sum(square, axis=1, keepdims=True) / count
+    return jnp.clip(jnp.floor(0.5 * jnp.log2(jnp.maximum(square, 1e-37))) - 1.0, -100.0, 100.0)
+
+
+def code(out, rows, square):
+    power = level(square, rows * out.shape[1])
+    scale = jnp.exp2(-power)
+
+    def slab(number, carry):
+        at = pl.ds(pl.multiple_of(number * SLAB, SLAB), SLAB)
+        value = out[at, :]
+        unit = jnp.abs(value) * scale
+        more = unit * unit + 1.0
+        grown = jnp.exp2(STRETCH * jnp.log2(unit + more * lax.rsqrt(more)) - 14.0)
+        out[at, :] = jnp.where(value < 0.0, -grown, grown)
+        return carry
+
+    lax.fori_loop(0, rows // SLAB, slab, 0)
     out[rows:, :] = jnp.broadcast_to(power, (EXTRA, out.shape[1]))
 
 
-def decoded(value):
-    rows = value.shape[0] - EXTRA
-    code = value[:rows, :]
-    grown = jnp.exp2((jnp.log2(jnp.abs(code)) + 14.0) * (1.0 / STRETCH))
-    unit = 0.5 * (grown - 1.0 / grown) * jnp.exp2(value[rows:rows + 1, :])
-    return jnp.where(code < 0.0, -unit, unit)
-
-
-def part_of(total, left, right, part, side):
+def decoded(value, scale):
+    lift = (jnp.log2(jnp.abs(value)) + 14.0) * (1.0 / STRETCH)
+    unit = (jnp.exp2(lift) - jnp.exp2(-lift)) * scale
+    return jnp.where(value < 0.0, -unit, unit)
+
+
+def part_of(total, left, right, part, start):
     rows = total.shape[0] // 4
     depth, width = right.shape
     at = pl.ds(part * rows, rows)
-    return total[at, side * width:(side + 1) * width] + jnp.dot(left[at, 3 * depth:], right[...], preferred_element_type=jnp.float32)
-
-
-def away_kernel(side, total, left, right, out):
-    coded(part_of(total, left, right, 0, side), out)
-
-
-def rest_kernel(side, total, left, right, out):
+    return total[at, start:start + width] + jnp.dot(left[at, 3 * depth:], right[...], preferred_element_type=jnp.float32)
+
+
+def away_kernel(start, total, left, right, out):
+    value = part_of(total, left, right, 0, start)
+    rows = value.shape[0]
+    out[:rows, :] = value
+    code(out, rows, jnp.sum(value * value, axis=0, keepdims=True))
+
+
+def rest_kernel(start, total, left, right, out):
     rows = total.shape[0] // 4
     for part in range(3):
-        out[part * rows:(part + 1) * rows, :] = part_of(total, left, right, part + 1, side)
-
-
-def last(kernel, rows, total, left, right, side):
+        out[part * rows:(part + 1) * rows, :] = part_of(total, left, right, part + 1, start)
+
+
+def last(kernel, rows, total, left, right, start):
     depth, width = right.shape
     flops = 2 * sum(rows) * depth * width
     return pl.pallas_call(
-        functools.partial(kernel, side),
+        functools.partial(kernel, start),
         out_shape=[pltpu.VMEM((count, width), jnp.float32) for count in rows],
         in_specs=[IN_VMEM] * 3,
         out_specs=[IN_VMEM] * len(rows),
@@ -192,11 +208,17 @@
 
 def more_kernel(first, base, value, out):
     rows = value.shape[0] - EXTRA
-    total = base[first:first + rows, :] + decoded(value)
+    scale = 0.5 * jnp.exp2(value[rows:rows + 1, :])
+
+    def slab(number, square):
+        start = pl.multiple_of(number * SLAB, SLAB)
+        total = base[pl.ds(first + start, SLAB), :] + decoded(value[pl.ds(start, SLAB), :], scale)
+        out[pl.ds(start, SLAB), :] = total
+        return square + jnp.sum(total * total, axis=0, keepdims=True)
+
+    square = lax.fori_loop(0, rows // SLAB, slab, jnp.zeros((1, out.shape[1]), jnp.float32))
     if out.shape[0] > rows:
-        coded(total, out)
-    else:
-        out[...] = total
+        code(out, rows, square)
 
 
 def more(base, first, value, extra):
@@ -237,7 +259,7 @@
     third = exchange(third_sent, Y, True)
     own_theirs = swap_cores(left_own)
     far_theirs = swap_cores(left_far)
-    middle = third.shape[1] // 2
+    middle = 640
     fourth = exchange(third[:, :middle], Y, False)
     fourth_right = exchange(third[:, middle:], Y, False)
     left = ordered(left_own, left_far, own_theirs, far_theirs)
@@ -245,8 +267,8 @@
     kept = []
     for side, columns in enumerate((fourth, fourth_right)):
         rows = total.shape[0] // 4
-        away, = last(away_kernel, (rows + EXTRA,), total, left, columns, side)
-        rest, = last(rest_kernel, (3 * rows,), total, left, columns, side)
+        away, = last(away_kernel, (rows + EXTRA,), total, left, columns, side * middle)
+        rest, = last(rest_kernel, (3 * rows,), total, left, columns, side * middle)
         far = more(rest, 0, sent(away, False), EXTRA)
         close = more(rest, rows, sent(far, True), EXTRA)
         own = more(rest, 2 * rows, sent(close, False), 0)

time: 143 us -> 146 us (1.021)
  the two profiles are of different devices: /device:TPU:32 before, /device:TPU:56 now
where the time goes in v3:
time: 146 us; the launch traced here: 145 us
  starting transfers between devices  73.7 us (50%)
  waiting for transfers between devices  54.6 us (37%)
  Pallas kernels  12.4 us (8%)
  local copies, waits for them, and re-layouts  2.36 us (2%)
    ppermute x17, starting transfers between devices, exchange(): return lax.ppermute(value, (*axes, CORE), pairs)  62.5 us
    ppermute x17, waiting for transfers between devices, exchange(): return lax.ppermute(value, (*axes, CORE), pairs)  41.7 us
    ppermute x2, waiting for transfers between devices, swap_high(): return lax.ppermute(value, ('row_1',), [(0, 1), (1, 0)])  12.9 us
    ppermute x2, starting transfers between devices, swap_high(): return lax.ppermute(value, ('row_1',), [(0, 1), (1, 0)])  6.85 us
    ppermute x2, starting transfers between devices, swap_cores(): return lax.ppermute(value, (CORE,), [(0, 1), (1, 0)])  4.33 us
    pallas_call x6, Pallas kernels, more(): pl.pallas_call(functools.partial(more_kernel, first), out_shape=pltpu.VME...  4.29 us
    pallas_call x1, Pallas kernels, most(): pl.pallas_call(most_kernel, out_shape=pltpu.VMEM((rows, width), jnp.float...  3.44 us
    pallas_call x4, Pallas kernels, last(): pl.pallas_call(functools.partial(kernel, start), out_shape=[pltpu.VMEM((c...  2.96 us
  transfers between devices with their start and end apart: 21, of which 13 were waited for; matrix products, arithmetic and copies ran while one was open for 1% of the time, Pallas kernels for 9%

profile of v3, /device:TPU:56, one launch (start us, length us, event | category | flops | bytes accessed | tf_op | source)
XLA Modules:
  0.0 145.0 jit_solution(13145079014601032676)
XLA Ops:
  1.1 4.9 %collective-permute-start = (bf16[128,1024]{1,0:T(8,128)(2,1)S(1)}, bf16[128,1024]{1,0:T(8,128)(2,1)S(1)}, u32[]{:S(2)}, u32[]{:S(2)}) collective-permute-start(bf16[128,1024]{1,0:T(8,128)(2,1)S(1)} %get-tuple-element.10), channel_id=1, source_target_pairs={{0,4},{4,0},{1,5},{5,1},{2,6},{6,2},{3,7},{7,3},{8,12},{12,8},{9,1... | collective-permute-start | bytes 786440 | tf_op jit(solution)/shard_map/ppermute | solution.py:58
  6.0 6.5 %collective-permute-done = bf16[128,1024]{1,0:T(8,128)(2,1)S(1)} collective-permute-done((bf16[128,1024]{1,0:T(8,128)(2,1)S(1)}, bf16[128,1024]{1,0:T(8,128)(2,1)S(1)}, u32[]{:S(2)}, u32[]{:S(2)}) %collective-permute-start) | collective-permute-done | bytes 262176 | tf_op jit(solution)/shard_map/ppermute | solution.py:58
  12.5 3.4 %collective-permute-start.1 = (bf16[512,512]{1,0:T(8,128)(2,1)}, bf16[512,512]{1,0:T(8,128)(2,1)S(1)}, u32[]{:S(2)}, u32[]{:S(2)}) collective-permute-start(bf16[512,512]{1,0:T(8,128)(2,1)} %param.2), channel_id=1, source_target_pairs={{0,2},{1,7},{2,0},{3,5},{4,6},{5,3},{6,4},{7,1},{8,10},{9,15},{10,... | collective-permute-start | bytes 1572872 | tf_op jit(solution)/shard_map/ppermute | solution.py:44
  15.9 3.3 %collective-permute-start.5 = (bf16[128,1024]{1,0:T(8,128)(2,1)S(1)}, bf16[128,1024]{1,0:T(8,128)(2,1)S(1)}, u32[]{:S(2)}, u32[]{:S(2)}) collective-permute-start(bf16[128,1024]{1,0:T(8,128)(2,1)S(1)} %get-tuple-element.9), channel_id=1, source_target_pairs={{0,8},{1,57},{8,0},{9,17},{16,24},{17,9},{24,16},{25,33},{32,40},{... | collective-permute-start | bytes 786440 | tf_op jit(solution)/shard_map/ppermute | solution.py:44
  19.2 2.6 %collective-permute-start.6 = (bf16[128,1024]{1,0:T(8,128)(2,1)S(1)}, bf16[128,1024]{1,0:T(8,128)(2,1)S(1)}, u32[]{:S(2)}, u32[]{:S(2)}) collective-permute-start(bf16[128,1024]{1,0:T(8,128)(2,1)S(1)} %collective-permute-done), channel_id=1, source_target_pairs={{0,8},{1,57},{8,0},{9,17},{16,24},{17,9},{24,16},{25,33},{32,40},{... | collective-permute-start | bytes 786440 | tf_op jit(solution)/shard_map/ppermute | solution.py:44
  24.3 4.2 %collective-permute-start.2 = (bf16[1024,512]{1,0:T(8,128)(2,1)S(1)}, bf16[1024,512]{1,0:T(8,128)(2,1)S(1)}, u32[]{:S(2)}, u32[]{:S(2)}) collective-permute-start(bf16[1024,512]{1,0:T(8,128)(2,1)S(1)} %constant_dynamic-update-slice_fusion.own), channel_id=1, source_target_pairs={{0,6},{1,3},{2,4},{3,1},{4,2},{5,7},{6,0},{7,5},{8,14},{9,11},{10,... | collective-permute-start | bytes 3145736 | tf_op jit(solution)/shard_map/ppermute | solution.py:44
  28.5 2.6 %collective-permute-start.7 = (bf16[256,1024]{1,0:T(8,128)(2,1)S(1)}, bf16[256,1024]{1,0:T(8,128)(2,1)S(1)}, u32[]{:S(2)}, u32[]{:S(2)}) collective-permute-start(bf16[256,1024]{1,0:T(8,128)(2,1)S(1)} %pad_maximum_fusion.1.first), channel_id=1, source_target_pairs={{0,56},{1,9},{8,16},{9,1},{16,8},{17,25},{24,32},{25,17},{32,24},{... | collective-permute-start | bytes 1572872 | tf_op jit(solution)/shard_map/ppermute | solution.py:44
  31.2 4.5 %collective-permute-start.8 = (bf16[256,1024]{1,0:T(8,128)(2,1)S(1)}, bf16[256,1024]{1,0:T(8,128)(2,1)S(1)}, u32[]{:S(2)}, u32[]{:S(2)}) collective-permute-start(bf16[256,1024]{1,0:T(8,128)(2,1)S(1)} %constant_dynamic-update-slice_fusion.2.first_2), channel_id=1, source_target_pairs={{0,56},{1,9},{8,16},{9,1},{16,8},{17,25},{24,32},{25,17},{32,24},{... | collective-permute-start | bytes 1572872 | tf_op jit(solution)/shard_map/ppermute | solution.py:44
  35.6 5.2 %collective-permute-done.7.second = bf16[256,1024]{1,0:T(8,128)(2,1)S(1)} collective-permute-done((bf16[256,1024]{1,0:T(8,128)(2,1)S(1)}, bf16[256,1024]{1,0:T(8,128)(2,1)S(1)}, u32[]{:S(2)}, u32[]{:S(2)}) %collective-permute-start.7) | collective-permute-done | bytes 524320 | tf_op jit(solution)/shard_map/ppermute | solution.py:44
  40.8 5.6 %collective-permute-done.8.second_2 = bf16[256,1024]{1,0:T(8,128)(2,1)S(1)} collective-permute-done((bf16[256,1024]{1,0:T(8,128)(2,1)S(1)}, bf16[256,1024]{1,0:T(8,128)(2,1)S(1)}, u32[]{:S(2)}, u32[]{:S(2)}) %collective-permute-start.8) | collective-permute-done | bytes 524320 | tf_op jit(solution)/shard_map/ppermute | solution.py:44
  50.5 2.4 %collective-permute-start.4 = (bf16[1024,512]{1,0:T(8,128)(2,1)S(1)}, bf16[1024,512]{1,0:T(8,128)(2,1)S(1)}, u32[]{:S(2)}, u32[]{:S(2)}) collective-permute-start(bf16[1024,512]{1,0:T(8,128)(2,1)S(1)} %collective-permute-done.2.far), channel_id=1, source_target_pairs={{0,1},{1,0},{2,3},{3,2},{4,5},{5,4},{6,7},{7,6},{8,9},{9,8},{10,11... | collective-permute-start | bytes 3145736 | tf_op jit(solution)/shard_map/ppermute | solution.py:48
  52.9 10.3 %collective-permute-done.9.third = bf16[512,1024]{1,0:T(8,128)(2,1)S(1)} collective-permute-done((bf16[512,1024]{1,0:T(8,128)(2,1)S(1)}, bf16[512,1024]{1,0:T(8,128)(2,1)S(1)}, u32[]{:S(2)}, u32[]{:S(2)}) %collective-permute-start.9) | collective-permute-done | bytes 1048608 | tf_op jit(solution)/shard_map/ppermute | solution.py:44
  63.3 2.7 %collective-permute-start.10 = (bf16[512,640]{1,0:T(8,128)(2,1)S(1)}, bf16[512,640]{1,0:T(8,128)(2,1)S(1)}, u32[]{:S(2)}, u32[]{:S(2)}) collective-permute-start(bf16[512,640]{1,0:T(8,128)(2,1)S(1)} %slice.32), channel_id=1, source_target_pairs={{0,56},{1,9},{8,16},{9,1},{16,8},{17,25},{24,32},{25,17},{32,24},{... | collective-permute-start | bytes 1966088 | tf_op jit(solution)/shard_map/ppermute | solution.py:44
  66.0 4.3 %collective-permute-start.15 = (bf16[512,384]{1,0:T(8,128)(2,1)S(1)}, bf16[512,384]{1,0:T(8,128)(2,1)S(1)}, u32[]{:S(2)}, u32[]{:S(2)}) collective-permute-start(bf16[512,384]{1,0:T(8,128)(2,1)S(1)} %slice.35), channel_id=1, source_target_pairs={{0,56},{1,9},{8,16},{9,1},{16,8},{17,25},{24,32},{25,17},{32,24},{... | collective-permute-start | bytes 1179656 | tf_op jit(solution)/shard_map/ppermute | solution.py:44
  72.2 3.4 %most.1.total = f32[1024,1024]{1,0:T(8,128)S(1)} custom-call(bf16[1024,2048]{1,0:T(8,128)(2,1)S(1)} %order_left.1.left, bf16[256,1024]{1,0:T(8,128)(2,1)S(1)} %pad_maximum_fusion.1.first, bf16[256,1024]{1,0:T(8,128)(2,1)S(1)} %constant_dynamic-update-slice_fusion.2.first_2, bf16[256,1024]{1,0:T(8,128)(2,1)S(1)} %collective-permute-done.7.second, ...), custom_call_target="tpu_custom_call" | custom-call | flops 3221225472 | bytes 4194304 | tf_op jit(solution)/shard_map/most/pallas_call | solution.py:134
  77.9 10.9 %collective-permute-start.11 = (f16[272,640]{1,0:T(8,128)(2,1)S(1)}, f16[272,640]{1,0:T(8,128)(2,1)S(1)}, u32[]{:S(2)}, u32[]{:S(2)}) collective-permute-start(f16[272,640]{1,0:T(8,128)(2,1)S(1)} %convert_element_type.42), channel_id=1, source_target_pairs={{0,448},{1,65},{64,128},{65,1},{128,64},{129,193},{192,256},{193,1... | collective-permute-start | bytes 1044488 | tf_op jit(solution)/shard_map/ppermute | solution.py:44
  89.6 3.2 %collective-permute-start.16 = (f16[272,384]{1,0:T(8,128)(2,1)S(1)}, f16[272,384]{1,0:T(8,128)(2,1)S(1)}, u32[]{:S(2)}, u32[]{:S(2)}) collective-permute-start(f16[272,384]{1,0:T(8,128)(2,1)S(1)} %convert_element_type.49), channel_id=1, source_target_pairs={{0,448},{1,65},{64,128},{65,1},{128,64},{129,193},{192,256},{193,1... | collective-permute-start | bytes 626696 | tf_op jit(solution)/shard_map/ppermute | solution.py:44
  103.9 2.4 %collective-permute-done.12 = f16[272,640]{1,0:T(8,128)(2,1)S(1)} collective-permute-done((f16[272,640]{1,0:T(8,128)(2,1)S(1)}, f16[272,640]{1,0:T(8,128)(2,1)S(1)}, u32[]{:S(2)}, u32[]{:S(2)}) %collective-permute-start.12) | collective-permute-done | bytes 348192 | tf_op jit(solution)/shard_map/ppermute | solution.py:44
  107.3 5.2 %collective-permute-start.13 = (f16[272,640]{1,0:T(8,128)(2,1)S(1)}, f16[272,640]{1,0:T(8,128)(2,1)S(1)}, u32[]{:S(2)}, u32[]{:S(2)}) collective-permute-start(f16[272,640]{1,0:T(8,128)(2,1)S(1)} %convert_element_type.46), channel_id=1, source_target_pairs={{0,448},{1,65},{64,128},{65,1},{128,64},{129,193},{192,256},{193,1... | collective-permute-start | bytes 1044488 | tf_op jit(solution)/shard_map/ppermute | solution.py:44
  113.4 3.5 %collective-permute-start.18 = (f16[272,384]{1,0:T(8,128)(2,1)S(1)}, f16[272,384]{1,0:T(8,128)(2,1)S(1)}, u32[]{:S(2)}, u32[]{:S(2)}) collective-permute-start(f16[272,384]{1,0:T(8,128)(2,1)S(1)} %convert_element_type.53), channel_id=1, source_target_pairs={{0,448},{1,65},{64,128},{65,1},{128,64},{129,193},{192,256},{193,1... | collective-permute-start | bytes 626696 | tf_op jit(solution)/shard_map/ppermute | solution.py:44
  116.9 7.0 %collective-permute-done.18 = f16[272,384]{1,0:T(8,128)(2,1)S(1)} collective-permute-done((f16[272,384]{1,0:T(8,128)(2,1)S(1)}, f16[272,384]{1,0:T(8,128)(2,1)S(1)}, u32[]{:S(2)}, u32[]{:S(2)}) %collective-permute-start.18) | collective-permute-done | bytes 208928 | tf_op jit(solution)/shard_map/ppermute | solution.py:44
  126.8 3.9 %collective-permute-start.14 = (f32[128,640]{1,0:T(8,128)S(1)}, f32[128,640]{1,0:T(8,128)S(1)}, u32[]{:S(2)}, u32[]{:S(2)}) collective-permute-start(f32[128,640]{1,0:T(8,128)S(1)} %slice.34), channel_id=1, source_target_pairs={{0,64},{1,449},{64,0},{65,129},{128,192},{129,65},{192,128},{193,2... | collective-permute-start | bytes 983048 | tf_op jit(solution)/shard_map/ppermute | solution.py:44
  131.9 3.8 %collective-permute-done.14 = f32[128,640]{1,0:T(8,128)S(1)} collective-permute-done((f32[128,640]{1,0:T(8,128)S(1)}, f32[128,640]{1,0:T(8,128)S(1)}, u32[]{:S(2)}, u32[]{:S(2)}) %collective-permute-start.14) | collective-permute-done | bytes 327712 | tf_op jit(solution)/shard_map/ppermute | solution.py:44
  137.8 6.4 %collective-permute-done.20 = bf16[64,1024]{1,0:T(8,128)(2,1)S(1)} collective-permute-done((bf16[64,1024]{1,0:T(8,128)(2,1)S(1)}, bf16[64,1024]{1,0:T(8,128)(2,1)S(1)}, u32[]{:S(2)}, u32[]{:S(2)}) %collective-permute-start.20) | collective-permute-done | bytes 131104 | tf_op jit(solution)/shard_map/ppermute | solution.py:58
  (58 shorter events, 32.1 us)
Async XLA Ops:
  1.1 11.4 %collective-permute-start = (bf16[128,1024]{1,0:T(8,128)(2,1)S(1)}, bf16[128,1024]{1,0:T(8,128)(2,1)S(1)}, u32[]{:S(2)}, u32[]{:S(2)}) collective-permute-start(bf16[128,1024]{1,0:T(8,128)(2,1)S(1)} %get-tuple-element.10), channel_id=1, source_target_pairs={{0,4},{4,0},{1,5},{5,1},{2,6},{6,2},{3,7},{7,3},{8,12},{12,8},{9,1... | collective-permute-start | bytes 786440 | tf_op jit(solution)/shard_map/ppermute | solution.py:58
  12.5 11.7 %collective-permute-start.1 = (bf16[512,512]{1,0:T(8,128)(2,1)}, bf16[512,512]{1,0:T(8,128)(2,1)S(1)}, u32[]{:S(2)}, u32[]{:S(2)}) collective-permute-start(bf16[512,512]{1,0:T(8,128)(2,1)} %param.2), channel_id=1, source_target_pairs={{0,2},{1,7},{2,0},{3,5},{4,6},{5,3},{6,4},{7,1},{8,10},{9,15},{10,... | collective-permute-start | bytes 1572872 | tf_op jit(solution)/shard_map/ppermute | solution.py:44
  15.9 8.3 %collective-permute-start.5 = (bf16[128,1024]{1,0:T(8,128)(2,1)S(1)}, bf16[128,1024]{1,0:T(8,128)(2,1)S(1)}, u32[]{:S(2)}, u32[]{:S(2)}) collective-permute-start(bf16[128,1024]{1,0:T(8,128)(2,1)S(1)} %get-tuple-element.9), channel_id=1, source_target_pairs={{0,8},{1,57},{8,0},{9,17},{16,24},{17,9},{24,16},{25,33},{32,40},{... | collective-permute-start | bytes 786440 | tf_op jit(solution)/shard_map/ppermute | solution.py:44
  19.2 12.0 %collective-permute-start.6 = (bf16[128,1024]{1,0:T(8,128)(2,1)S(1)}, bf16[128,1024]{1,0:T(8,128)(2,1)S(1)}, u32[]{:S(2)}, u32[]{:S(2)}) collective-permute-start(bf16[128,1024]{1,0:T(8,128)(2,1)S(1)} %collective-permute-done), channel_id=1, source_target_pairs={{0,8},{1,57},{8,0},{9,17},{16,24},{17,9},{24,16},{25,33},{32,40},{... | collective-permute-start | bytes 786440 | tf_op jit(solution)/shard_map/ppermute | solution.py:44
  24.3 26.2 %collective-permute-start.2 = (bf16[1024,512]{1,0:T(8,128)(2,1)S(1)}, bf16[1024,512]{1,0:T(8,128)(2,1)S(1)}, u32[]{:S(2)}, u32[]{:S(2)}) collective-permute-start(bf16[1024,512]{1,0:T(8,128)(2,1)S(1)} %constant_dynamic-update-slice_fusion.own), channel_id=1, source_target_pairs={{0,6},{1,3},{2,4},{3,1},{4,2},{5,7},{6,0},{7,5},{8,14},{9,11},{10,... | collective-permute-start | bytes 3145736 | tf_op jit(solution)/shard_map/ppermute | solution.py:44
  28.5 12.3 %collective-permute-start.7 = (bf16[256,1024]{1,0:T(8,128)(2,1)S(1)}, bf16[256,1024]{1,0:T(8,128)(2,1)S(1)}, u32[]{:S(2)}, u32[]{:S(2)}) collective-permute-start(bf16[256,1024]{1,0:T(8,128)(2,1)S(1)} %pad_maximum_fusion.1.first), channel_id=1, source_target_pairs={{0,56},{1,9},{8,16},{9,1},{16,8},{17,25},{24,32},{25,17},{32,24},{... | collective-permute-start | bytes 1572872 | tf_op jit(solution)/shard_map/ppermute | solution.py:44
  31.2 15.3 %collective-permute-start.8 = (bf16[256,1024]{1,0:T(8,128)(2,1)S(1)}, bf16[256,1024]{1,0:T(8,128)(2,1)S(1)}, u32[]{:S(2)}, u32[]{:S(2)}) collective-permute-start(bf16[256,1024]{1,0:T(8,128)(2,1)S(1)} %constant_dynamic-update-slice_fusion.2.first_2), channel_id=1, source_target_pairs={{0,56},{1,9},{8,16},{9,1},{16,8},{17,25},{24,32},{25,17},{32,24},{... | collective-permute-start | bytes 1572872 | tf_op jit(solution)/shard_map/ppermute | solution.py:44
  46.5 16.7 %collective-permute-start.9 = (bf16[512,1024]{1,0:T(8,128)(2,1)S(1)}, bf16[512,1024]{1,0:T(8,128)(2,1)S(1)}, u32[]{:S(2)}, u32[]{:S(2)}) collective-permute-start(bf16[512,1024]{1,0:T(8,128)(2,1)S(1)} %pad_maximum_fusion), channel_id=1, source_target_pairs={{0,8},{1,57},{8,0},{9,17},{16,24},{17,9},{24,16},{25,33},{32,40},{... | collective-permute-start | bytes 3145736 | tf_op jit(solution)/shard_map/ppermute | solution.py:44
  48.6 21.8 %collective-permute-start.3 = (bf16[1024,512]{1,0:T(8,128)(2,1)S(1)}, bf16[1024,512]{1,0:T(8,128)(2,1)S(1)}, u32[]{:S(2)}, u32[]{:S(2)}) collective-permute-start(bf16[1024,512]{1,0:T(8,128)(2,1)S(1)} %constant_dynamic-update-slice_fusion.own), channel_id=1, source_target_pairs={{0,1},{1,0},{2,3},{3,2},{4,5},{5,4},{6,7},{7,6},{8,9},{9,8},{10,11... | collective-permute-start | bytes 3145736 | tf_op jit(solution)/shard_map/ppermute | solution.py:48
  50.5 19.9 %collective-permute-start.4 = (bf16[1024,512]{1,0:T(8,128)(2,1)S(1)}, bf16[1024,512]{1,0:T(8,128)(2,1)S(1)}, u32[]{:S(2)}, u32[]{:S(2)}) collective-permute-start(bf16[1024,512]{1,0:T(8,128)(2,1)S(1)} %collective-permute-done.2.far), channel_id=1, source_target_pairs={{0,1},{1,0},{2,3},{3,2},{4,5},{5,4},{6,7},{7,6},{8,9},{9,8},{10,11... | collective-permute-start | bytes 3145736 | tf_op jit(solution)/shard_map/ppermute | solution.py:48
  63.3 13.7 %collective-permute-start.10 = (bf16[512,640]{1,0:T(8,128)(2,1)S(1)}, bf16[512,640]{1,0:T(8,128)(2,1)S(1)}, u32[]{:S(2)}, u32[]{:S(2)}) collective-permute-start(bf16[512,640]{1,0:T(8,128)(2,1)S(1)} %slice.32), channel_id=1, source_target_pairs={{0,56},{1,9},{8,16},{9,1},{16,8},{17,25},{24,32},{25,17},{32,24},{... | collective-permute-start | bytes 1966088 | tf_op jit(solution)/shard_map/ppermute | solution.py:44
  66.0 22.8 %collective-permute-start.15 = (bf16[512,384]{1,0:T(8,128)(2,1)S(1)}, bf16[512,384]{1,0:T(8,128)(2,1)S(1)}, u32[]{:S(2)}, u32[]{:S(2)}) collective-permute-start(bf16[512,384]{1,0:T(8,128)(2,1)S(1)} %slice.35), channel_id=1, source_target_pairs={{0,56},{1,9},{8,16},{9,1},{16,8},{17,25},{24,32},{25,17},{32,24},{... | collective-permute-start | bytes 1179656 | tf_op jit(solution)/shard_map/ppermute | solution.py:44
  77.9 17.5 %collective-permute-start.11 = (f16[272,640]{1,0:T(8,128)(2,1)S(1)}, f16[272,640]{1,0:T(8,128)(2,1)S(1)}, u32[]{:S(2)}, u32[]{:S(2)}) collective-permute-start(f16[272,640]{1,0:T(8,128)(2,1)S(1)} %convert_element_type.42), channel_id=1, source_target_pairs={{0,448},{1,65},{64,128},{65,1},{128,64},{129,193},{192,256},{193,1... | collective-permute-start | bytes 1044488 | tf_op jit(solution)/shard_map/ppermute | solution.py:44
  89.6 11.1 %collective-permute-start.16 = (f16[272,384]{1,0:T(8,128)(2,1)S(1)}, f16[272,384]{1,0:T(8,128)(2,1)S(1)}, u32[]{:S(2)}, u32[]{:S(2)}) collective-permute-start(f16[272,384]{1,0:T(8,128)(2,1)S(1)} %convert_element_type.49), channel_id=1, source_target_pairs={{0,448},{1,65},{64,128},{65,1},{128,64},{129,193},{192,256},{193,1... | collective-permute-start | bytes 626696 | tf_op jit(solution)/shard_map/ppermute | solution.py:44
  96.6 9.6 %collective-permute-start.12 = (f16[272,640]{1,0:T(8,128)(2,1)S(1)}, f16[272,640]{1,0:T(8,128)(2,1)S(1)}, u32[]{:S(2)}, u32[]{:S(2)}) collective-permute-start(f16[272,640]{1,0:T(8,128)(2,1)S(1)} %convert_element_type.44), channel_id=1, source_target_pairs={{0,64},{1,449},{64,0},{65,129},{128,192},{129,65},{192,128},{193,2... | collective-permute-start | bytes 1044488 | tf_op jit(solution)/shard_map/ppermute | solution.py:44
  101.6 11.0 %collective-permute-start.17 = (f16[272,384]{1,0:T(8,128)(2,1)S(1)}, f16[272,384]{1,0:T(8,128)(2,1)S(1)}, u32[]{:S(2)}, u32[]{:S(2)}) collective-permute-start(f16[272,384]{1,0:T(8,128)(2,1)S(1)} %convert_element_type.51), channel_id=1, source_target_pairs={{0,64},{1,449},{64,0},{65,129},{128,192},{129,65},{192,128},{193,2... | collective-permute-start | bytes 626696 | tf_op jit(solution)/shard_map/ppermute | solution.py:44
  107.3 18.9 %collective-permute-start.13 = (f16[272,640]{1,0:T(8,128)(2,1)S(1)}, f16[272,640]{1,0:T(8,128)(2,1)S(1)}, u32[]{:S(2)}, u32[]{:S(2)}) collective-permute-start(f16[272,640]{1,0:T(8,128)(2,1)S(1)} %convert_element_type.46), channel_id=1, source_target_pairs={{0,448},{1,65},{64,128},{65,1},{128,64},{129,193},{192,256},{193,1... | collective-permute-start | bytes 1044488 | tf_op jit(solution)/shard_map/ppermute | solution.py:44
  113.4 10.5 %collective-permute-start.18 = (f16[272,384]{1,0:T(8,128)(2,1)S(1)}, f16[272,384]{1,0:T(8,128)(2,1)S(1)}, u32[]{:S(2)}, u32[]{:S(2)}) collective-permute-start(f16[272,384]{1,0:T(8,128)(2,1)S(1)} %convert_element_type.53), channel_id=1, source_target_pairs={{0,448},{1,65},{64,128},{65,1},{128,64},{129,193},{192,256},{193,1... | collective-permute-start | bytes 626696 | tf_op jit(solution)/shard_map/ppermute | solution.py:44
  124.3 7.6 %collective-permute-start.19 = (f32[128,384]{1,0:T(8,128)S(1)}, f32[128,384]{1,0:T(8,128)S(1)}, u32[]{:S(2)}, u32[]{:S(2)}) collective-permute-start(f32[128,384]{1,0:T(8,128)S(1)} %slice.37), channel_id=1, source_target_pairs={{0,64},{1,449},{64,0},{65,129},{128,192},{129,65},{192,128},{193,2... | collective-permute-start | bytes 589832 | tf_op jit(solution)/shard_map/ppermute | solution.py:44
  126.8 9.0 %collective-permute-start.14 = (f32[128,640]{1,0:T(8,128)S(1)}, f32[128,640]{1,0:T(8,128)S(1)}, u32[]{:S(2)}, u32[]{:S(2)}) collective-permute-start(f32[128,640]{1,0:T(8,128)S(1)} %slice.34), channel_id=1, source_target_pairs={{0,64},{1,449},{64,0},{65,129},{128,192},{129,65},{192,128},{193,2... | collective-permute-start | bytes 983048 | tf_op jit(solution)/shard_map/ppermute | solution.py:44
  135.8 8.4 %collective-permute-start.20 = (bf16[64,1024]{1,0:T(8,128)(2,1)S(1)}, bf16[64,1024]{1,0:T(8,128)(2,1)S(1)}, u32[]{:S(2)}, u32[]{:S(2)}) collective-permute-start(bf16[64,1024]{1,0:T(8,128)(2,1)S(1)} %pad_maximum_fusion.3), channel_id=1, source_target_pairs={{0,4},{4,0},{1,5},{5,1},{2,6},{6,2},{3,7},{7,3},{8,12},{12,8},{9,1... | collective-permute-start | bytes 393224 | tf_op jit(solution)/shard_map/ppermute | solution.py:58
